TPU v7x, 128 devices: a whole 4x4x4 slice. The times are simulated.
128 devices in a mesh: seq: 32 (over y, z_hi, x), head: 4 (over z_lo, core).
Axes of the slice: x: 4, y: 4, z: 4 (z_hi: 2, z_lo: 2; z = z_hi * 2 + z_lo), core: 2. Of those that a mesh axis runs over, the one named last changes fastest.
Arguments:
- hidden: bfloat16 [4096, 3072], P('seq'), may hold values from -6 to 6
- cotangent: bfloat16 [4096, 3072], P('seq'), may hold values from -6 to 6
- mod_scale: float32 [3072], replicated, may hold values from -0.5 to 0.5
- mod_shift: float32 [3072], replicated, may hold values from -3 to 3
- branch_gate: float32 [3072], replicated, may hold values from 0.3 to 1.5
- query_weight: bfloat16 [3072, 1536], P('seq', 'head'), may hold values from -0.108253175 to 0.108253175, as said below
- key_weight: bfloat16 [3072, 1536], P('seq', 'head'), may hold values from -0.108253175 to 0.108253175, as said below
- value_weight: bfloat16 [3072, 1536], P('seq', 'head'), may hold values from -0.109375 to 0.109375
- output_weight: bfloat16 [3072, 1536], P('seq', 'head'), may hold values from -0.15625 to 0.15625
- query_gain: float32 [1536], P('head'), may hold values from 0.7 to 6.3
- key_gain: float32 [1536], P('head'), may hold values from 0.7 to 6.3
Outputs:
- hidden_grad: bfloat16 [4096, 3072], P('seq')
- outproj_grad: float32 [3072, 1536], P('seq', 'head')
Inputs may be any that keep to these rules, and one draw needn't show every extreme that they name: `query_weight`: entries of the query projection, of order 3072^-0.5. `key_weight`: entries of the key projection, of order 3072^-0.5.
All inputs are finite; a program needn't handle non-finite values.
Results may differ from a plain program's by a relative error of at most 0.028.
Values may be sent and summed in bfloat16 or wider, within the bound.
No kernel may reach another device: no remote copies, remote signals or barrier semaphores. Data moves between devices by JAX's collectives and lax.ppermute only.
A program may use at most 128 MiB of HBM per device.

v0:
```python
import math

import jax
import jax.numpy as jnp
from jax import lax
from jax.experimental import pallas as pl
from jax.experimental.pallas import tpu as pltpu
from jax.sharding import Mesh
from jax.sharding import PartitionSpec as P

HEAD_DIM = 128
SEQ = ("y", "z", "x")
EPSILON = 1e-06
FACTOR = 1.0 / math.sqrt(HEAD_DIM)
ROLES = 4
GRAD_ROLE = 3
TILE = 256
F32 = jnp.float32
BF16 = jnp.bfloat16


def nt(a, b):
    return lax.dot_general(a, b, (((1,), (1,)), ((), ())), preferred_element_type=F32)


def nn(a, b):
    return lax.dot_general(a, b, (((1,), (0,)), ((), ())), preferred_element_type=F32)


def shifted(array, axis, shift, sources=None):
    peers = lax.axis_size(axis)
    sources = range(peers) if sources is None else sources
    return lax.ppermute(array, axis, [(i, (i + shift) % peers) for i in sources])


def exchanged(array, axes):
    return lax.all_to_all(array, axes, 0, 0, tiled=True)


def call(kernel, outs, scratch=(), scalars=1):
    def run(*args):
        specs = [pl.BlockSpec(memory_space=pltpu.SMEM)] * scalars
        specs += [pl.BlockSpec(memory_space=pltpu.VMEM)] * (len(args) - scalars)
        return pl.pallas_call(
            kernel,
            out_shape=tuple(jax.ShapeDtypeStruct(s, t) for s, t in outs),
            in_specs=specs,
            out_specs=tuple(pl.BlockSpec(memory_space=pltpu.VMEM) for _ in outs),
            scratch_shapes=list(scratch),
            compiler_params=pltpu.CompilerParams(vmem_limit_bytes=56 * 1024 * 1024),
        )(*args)

    return run


def half_start(core, half):
    return pl.multiple_of(core * half, half)


def pack_kernel(query, key, value, output, packed):
    for h in range(GRAD_ROLE):
        at = slice(h * HEAD_DIM, (h + 1) * HEAD_DIM)
        for n, source in enumerate((query, key, value)):
            packed[h, :, n * HEAD_DIM : (n + 1) * HEAD_DIM] = source[:, at]
    packed[GRAD_ROLE] = output[...]


def norm_kernel(at, hidden, cot, scale, shift, gate, own, s1, s2, s3, c0, c1, c2, c3):
    y, core = at[0], at[1]
    values = hidden[...].astype(F32)
    center = values - jnp.mean(values, axis=-1, keepdims=True)
    inverse = lax.rsqrt(jnp.mean(center * center, axis=-1, keepdims=True) + EPSILON)
    normed = (center * inverse * (1.0 + scale[...]) + shift[...]).astype(BF16)
    graded = (cot[...].astype(F32) * gate[...]).astype(BF16)
    quarter = c0.shape[1]
    for n in range(ROLES):
        for j, part in enumerate((c0, c1, c2, c3)):

            @pl.when(lax.rem(y + j, ROLES) == n)
            def _():
                part[...] = graded[:, n * quarter : (n + 1) * quarter]

    own[...] = jnp.where(y == GRAD_ROLE, graded, normed)
    half = s1.shape[1]
    for j, sent in ((1, s1), (2, s2), (3, s3)):
        wanted = lax.rem(y + j, ROLES) == GRAD_ROLE

        @pl.when(core == 0)
        def _():
            sent[...] = jnp.where(wanted, graded[:, :half], normed[:, :half])

        @pl.when(core == 1)
        def _():
            sent[...] = jnp.where(wanted, graded[:, half:], normed[:, half:])


def project_kernel(
    at, own, m1, m2, m3, o1, o2, o3, pieces, gains, q_out, kv_out, raw_out, g0, g1, g2, weight
):
    y, core = at[0], at[1]
    groups, _, block, _ = pieces.shape
    for n in range(groups):
        for k in range(ROLES):
            at_row = (k * groups + n) * block
            weight[at_row : at_row + block, :] = pieces[n, k]
    half = m1.shape[1]
    here, there = half_start(core, half), half_start(1 - core, half)
    mine = jnp.concatenate([own[:, pl.ds(here, half)], m1[...], m2[...], m3[...]], axis=0)
    other = jnp.concatenate([own[:, pl.ds(there, half)], o1[...], o2[...], o3[...]], axis=0)
    total = nn(mine, weight[pl.ds(here, half), :]) + nn(other, weight[pl.ds(there, half), :])
    plain = y == GRAD_ROLE
    for at_column, gain, factor, out, column in (
        (0, 0, FACTOR, q_out, 0),
        (1, 1, 1.0, kv_out, 0),
    ):
        raw = total[:, at_column * HEAD_DIM : (at_column + 1) * HEAD_DIM]
        inverse = lax.rsqrt(jnp.mean(raw * raw, axis=-1, keepdims=True) + EPSILON)
        headed = raw * inverse * gains[gain : gain + 1, :] * factor
        out[:, column : column + HEAD_DIM] = jnp.where(plain, raw, headed).astype(BF16)
    kv_out[:, HEAD_DIM:] = total[:, 2 * HEAD_DIM :].astype(BF16)
    raw_out[...] = total[:, : 2 * HEAD_DIM]
    rows = own.shape[0]
    for h, out in enumerate((g0, g1, g2)):
        for j in range(ROLES):
            i = (GRAD_ROLE - h + j) % ROLES
            piece = total[i * rows : (i + 1) * rows, h * HEAD_DIM : (h + 1) * HEAD_DIM]
            out[j * rows : (j + 1) * rows, :] = piece.astype(BF16)


def stats_kernel(q0, q1, g0, g1, kv0, kv1, kv2, kv3, stats, mix_own, mix_other, q_all, g_all):
    rows = q0.shape[0]
    q_all[:rows, :] = q0[...]
    q_all[rows:, :] = q1[...]
    g_all[:rows, :] = g0[...]
    g_all[rows:, :] = g1[...]
    pieces = (kv0, kv1, kv2, kv3)
    keys = jnp.concatenate([p[:, :HEAD_DIM] for p in pieces], axis=0)
    values = jnp.concatenate([p[:, HEAD_DIM:] for p in pieces], axis=0)
    values_t = jnp.transpose(values)
    for half, mixed in ((0, mix_own), (1, mix_other)):

        def step(i, carry):
            at = pl.multiple_of(half * rows + i * TILE, TILE)
            local = pl.multiple_of(i * TILE, TILE)
            query = q_all[pl.ds(at, TILE), :]
            grad = g_all[pl.ds(at, TILE), :]
            scores = nt(keys, query)
            top = jnp.max(scores, axis=0, keepdims=True)
            expo = jnp.exp(scores - top)
            total = jnp.sum(expo, axis=0, keepdims=True)
            mix_t = nn(values_t, expo.astype(BF16))
            grad_t = jnp.transpose(grad.astype(F32))
            delta = jnp.sum(mix_t * grad_t, axis=0, keepdims=True)
            stats[0:1, pl.ds(at, TILE)] = top
            stats[1:2, pl.ds(at, TILE)] = total
            stats[2:3, pl.ds(at, TILE)] = delta
            mixed[:, pl.ds(local, TILE)] = mix_t.astype(mixed.dtype)
            return carry

        lax.fori_loop(0, rows // TILE, step, 0)
    stats[3:8, :] = jnp.zeros((5, stats.shape[1]), F32)


def combined(mine, theirs):
    top = jnp.maximum(mine[0:1, :], theirs[0:1, :])
    a, b = jnp.exp(mine[0:1, :] - top), jnp.exp(theirs[0:1, :] - top)
    total = mine[1:2, :] * a + theirs[1:2, :] * b
    delta = (mine[2:3, :] * a + theirs[2:3, :] * b) / total
    return (top, total, delta, a, b)


def grads_kernel(
    q0, q1, g0, g1, kv0, kv1, kv2, kv3, stats, sent, dq0, dq1, dkv0, dkv1, dkv2, dkv3,
    q_all, g_all, level, key_acc, value_acc, query_acc,
):
    rows = q0.shape[0]
    q_all[:rows, :] = q0[...]
    q_all[rows:, :] = q1[...]
    g_all[:rows, :] = g0[...]
    g_all[rows:, :] = g1[...]
    for here, there in ((0, rows), (rows, 0)):
        top, total, delta, _, _ = combined(stats[:, here : here + rows], sent[:, there : there + rows])
        level[0:1, here : here + rows] = top + jnp.log(total)
        level[1:2, here : here + rows] = delta
    pieces = (kv0, kv1, kv2, kv3)
    keys = jnp.concatenate([p[:, :HEAD_DIM] for p in pieces], axis=0)
    values = jnp.concatenate([p[:, HEAD_DIM:] for p in pieces], axis=0)
    keys_t = jnp.transpose(keys)
    key_acc[...] = jnp.zeros(key_acc.shape, F32)
    value_acc[...] = jnp.zeros(value_acc.shape, F32)

    def step(i, carry):
        at = pl.multiple_of(i * TILE, TILE)
        query = q_all[pl.ds(at, TILE), :]
        grad = g_all[pl.ds(at, TILE), :]
        probs = jnp.exp(nt(keys, query) - level[0:1, pl.ds(at, TILE)])
        score_grad = (probs * (nt(values, grad) - level[1:2, pl.ds(at, TILE)])).astype(BF16)
        value_acc[...] += nn(probs.astype(BF16), grad)
        key_acc[...] += nn(score_grad, query)
        query_acc[pl.ds(at, TILE), :] = jnp.transpose(nn(keys_t, score_grad))
        return carry

    lax.fori_loop(0, 2 * rows // TILE, step, 0)
    dq0[...] = query_acc[:rows, :]
    dq1[...] = query_acc[rows:, :].astype(BF16)
    for n, out in enumerate((dkv0, dkv1, dkv2, dkv3)):
        at = slice(n * rows, (n + 1) * rows)
        out[:, :HEAD_DIM] = key_acc[at, :].astype(out.dtype)
        out[:, HEAD_DIM:] = value_acc[at, :].astype(out.dtype)


def mix_kernel(stats, sent, own, other, m0, m1, m2, m3):
    rows = own.shape[1]
    _, total, _, a, b = combined(stats[:, :rows], sent[:, rows:])
    mixed = jnp.transpose((own[...] * a + other[...].astype(F32) * b) / total).astype(BF16)
    block = rows // ROLES
    for shift, out in enumerate((m0, m1, m2, m3)):
        for j in range(ROLES):
            i = (j - shift) % ROLES
            out[j * block : (j + 1) * block, :] = mixed[i * block : (i + 1) * block, :]


def outproj_kernel(at, m0, m1, m2, m3, c0, c1, c2, c3, out, mixes):
    y = at[0]
    for shift, part in enumerate((m0, m1, m2, m3)):
        head = lax.rem(y + ROLES - shift, ROLES)
        mixes[:, pl.ds(pl.multiple_of(head * HEAD_DIM, HEAD_DIM), HEAD_DIM)] = part[...]
    cot = jnp.concatenate([c0[...], c1[...], c2[...], c3[...]], axis=0)
    total = nn(jnp.transpose(cot), mixes[:, : GRAD_ROLE * HEAD_DIM]).astype(BF16)
    block = out.shape[1]
    for n in range(out.shape[0]):
        out[n] = total[n * block : (n + 1) * block, :]


def sum_kernel(parts, out):
    total = parts[0].astype(F32)
    for n in range(1, parts.shape[0]):
        total = total + parts[n].astype(F32)
    out[...] = total


def head_back(grad, raw, gain, factor):
    inverse = lax.rsqrt(jnp.mean(raw * raw, axis=-1, keepdims=True) + EPSILON)
    unit = raw * inverse
    scaled = grad * gain * factor
    along = jnp.mean(scaled * unit, axis=-1, keepdims=True)
    return (inverse * (scaled - unit * along)).astype(BF16)


def back_kernel(at, dq0, dq1, dkv0, dkv1, dkv2, dkv3, raw, gains, weight, kept, sent):
    y, core = at[0], at[1]
    half = kept.shape[1]
    here, there = half_start(core, half), half_start(1 - core, half)
    query_grad = dq0[...] + dq1[...].astype(F32)
    both = dkv0[...] + dkv1[...].astype(F32) + dkv2[...].astype(F32) + dkv3[...].astype(F32)
    query_raw = head_back(query_grad, raw[:, :HEAD_DIM], gains[0:1, :], FACTOR)
    key_raw = head_back(both[:, :HEAD_DIM], raw[:, HEAD_DIM:], gains[1:2, :], 1.0)
    value_raw = both[:, HEAD_DIM:].astype(BF16)
    grads = jnp.concatenate([query_raw, key_raw, value_raw], axis=1)
    grads = jnp.where(y == GRAD_ROLE, jnp.zeros_like(grads), grads)
    sent[...] = nt(grads, weight[pl.ds(there, half), :]).astype(BF16)
    kept[...] = nt(grads, weight[pl.ds(here, half), :]).astype(BF16)


def pair_kernel(kept, got, p0, p1, p2, p3):
    block = p0.shape[0]
    for n, out in enumerate((p0, p1, p2, p3)):
        at = slice(n * block, (n + 1) * block)
        out[...] = (kept[at, :].astype(F32) + got[at, :].astype(F32)).astype(BF16)


def line_kernel(p0, p1, p2, p3, out):
    total = p0[...].astype(F32) + p1[...].astype(F32) + p2[...].astype(F32) + p3[...].astype(F32)
    out[...] = total.astype(BF16)


def last_kernel(at, hidden, mine, other, scale, out, grad):
    half = mine.shape[1]
    here, there = half_start(at[1], half), half_start(1 - at[1], half)
    grad[:, pl.ds(here, half)] = mine[...].astype(F32)
    grad[:, pl.ds(there, half)] = other[...].astype(F32)
    values = hidden[...].astype(F32)
    center = values - jnp.mean(values, axis=-1, keepdims=True)
    inverse = lax.rsqrt(jnp.mean(center * center, axis=-1, keepdims=True) + EPSILON)
    unit = center * inverse
    scaled = grad[...] * (1.0 + scale[...])
    middle = jnp.mean(scaled, axis=-1, keepdims=True)
    along = jnp.mean(scaled * unit, axis=-1, keepdims=True)
    out[...] = (inverse * (scaled - middle - unit * along)).astype(BF16)


def body(
    hidden,
    cotangent,
    mod_scale,
    mod_shift,
    branch_gate,
    query_weight,
    key_weight,
    value_weight,
    output_weight,
    query_gain,
    key_gain,
):
    rows, width = hidden.shape
    half = width // 2
    line = ROLES * rows
    own_rows = query_weight.shape[0]
    columns = 3 * HEAD_DIM
    y = lax.axis_index("y")
    at = jnp.stack([y, lax.axis_index("core")]).astype(jnp.int32)
    scale, shift, gate = mod_scale[None], mod_shift[None], branch_gate[None]
    gains = jnp.stack(
        [lax.dynamic_slice_in_dim(g, y * HEAD_DIM, HEAD_DIM) for g in (query_gain, key_gain)]
    )

    (packed,) = call(pack_kernel, [((ROLES, own_rows, columns), BF16)], (), 0)(
        query_weight, key_weight, value_weight, output_weight
    )
    packed = exchanged(packed, "y")
    packed = jnp.broadcast_to(packed[None], (8, *packed.shape))
    pieces = exchanged(packed, ("z", "x"))

    own, s1, s2, s3, *cots = call(
        norm_kernel,
        [((rows, width), BF16)] + [((rows, half), BF16)] * 3 + [((rows, width // ROLES), BF16)] * 4,
    )(at, hidden, cotangent, scale, shift, gate)
    mine = [shifted(s, "y", j) for j, s in ((1, s1), (2, s2), (3, s3))]
    other = [shifted(m, "core", 1) for m in mine]
    query, kv, raw, *grad_sent, weight = call(
        project_kernel,
        [((line, HEAD_DIM), BF16), ((line, 2 * HEAD_DIM), BF16), ((line, 2 * HEAD_DIM), F32)]
        + [((line, HEAD_DIM), BF16)] * 3
        + [((width, columns), BF16)],
    )(at, own, *mine, *other, pieces, gains)

    kvs = [kv] + [shifted(kv, "x", j) for j in (1, 2, 3)]
    query_there = shifted(query, "z", 1)
    got = [shifted(g, "y", h - GRAD_ROLE, [GRAD_ROLE]) for h, g in enumerate(grad_sent)]
    grad = got[0] + got[1] + got[2]
    grad_there = shifted(grad, "z", 1)

    both = 2 * line
    stats, mix_own, mix_there = call(
        stats_kernel,
        [((8, both), F32), ((HEAD_DIM, line), F32), ((HEAD_DIM, line), BF16)],
        [pltpu.VMEM((both, HEAD_DIM), BF16), pltpu.VMEM((both, HEAD_DIM), BF16)],
        0,
    )(query, query_there, grad, grad_there, *kvs)
    sent_stats = shifted(stats, "z", 1)
    mix_got = shifted(mix_there, "z", 1)
    dq0, dq1, *dkvs = call(
        grads_kernel,
        [((line, HEAD_DIM), F32), ((line, HEAD_DIM), BF16), ((line, 2 * HEAD_DIM), F32)]
        + [((line, 2 * HEAD_DIM), BF16)] * 3,
        [
            pltpu.VMEM((both, HEAD_DIM), BF16),
            pltpu.VMEM((both, HEAD_DIM), BF16),
            pltpu.VMEM((8, both), F32),
            pltpu.VMEM((4 * line, HEAD_DIM), F32),
            pltpu.VMEM((4 * line, HEAD_DIM), F32),
            pltpu.VMEM((both, HEAD_DIM), F32),
        ],
        0,
    )(query, query_there, grad, grad_there, *kvs, stats, sent_stats)
    dq_got = shifted(dq1, "z", 1)
    dkv_got = [shifted(d, "x", -j) for j, d in zip((1, 2, 3), dkvs[1:])]

    cots = [cots[0]] + [shifted(c, "y", j) for j, c in zip((1, 2, 3), cots[1:])]
    mixes = call(mix_kernel, [((line, HEAD_DIM), BF16)] * 4, (), 0)(stats, sent_stats, mix_own, mix_got)
    mixes = [mixes[0]] + [shifted(m, "y", j, range(3)) for j, m in zip((1, 2, 3), mixes[1:])]
    (partial,) = call(
        outproj_kernel, [((8, own_rows, columns), BF16)], [pltpu.VMEM((line, ROLES * HEAD_DIM), BF16)]
    )(at, *mixes, *cots)
    partial = exchanged(partial, ("z", "x"))
    (outproj_grad,) = call(sum_kernel, [((own_rows, columns), F32)], (), 0)(partial)

    kept, sent = call(back_kernel, [((line, half), BF16)] * 2)(
        at, dq0, dq_got, dkvs[0], *dkv_got, raw, gains, weight
    )
    got = shifted(sent, "core", 1)
    parts = call(pair_kernel, [((rows, half), BF16)] * 4, (), 0)(kept, got)
    parts = [parts[0]] + [shifted(p, "y", -j, range(3)) for j, p in zip((1, 2, 3), parts[1:])]
    (chip,) = call(line_kernel, [((rows, half), BF16)], (), 0)(*parts)
    chip_got = shifted(chip, "zlo", 1)
    total = (chip.astype(F32) + chip_got.astype(F32)).astype(BF16)
    total_other = shifted(total, "core", 1)
    (hidden_grad,) = call(
        last_kernel, [((rows, width), BF16)], [pltpu.VMEM((rows, width), F32)]
    )(at, hidden, total, total_other, scale)
    return (hidden_grad, outproj_grad)


def solution(mesh):
    torus = Mesh(mesh.devices.reshape(4, 2, 4, 2, 2), ("y", "z", "x", "zlo", "core"))
    head = ("zlo", "core")
    return jax.shard_map(
        body,
        mesh=torus,
        in_specs=(
            P(SEQ, None),
            P(SEQ, None),
            P(),
            P(),
            P(),
            P(SEQ, head),
            P(SEQ, head),
            P(SEQ, head),
            P(SEQ, head),
            P(head),
            P(head),
        ),
        out_specs=(P(SEQ, None), P(SEQ, head)),
        check_vma=False,
    )
```

profile of v0, /device:TPU:1, one launch (start us, length us, event | category | flops | bytes accessed | tf_op | source)
XLA Modules:
  0.0 216.8 jit_solution(15032167248101659523)
XLA Ops:
  0.6 1.8 shard_map.123
  2.4 10.9 %all_to_all.15 = bf16[4,96,384]{2,1,0:T(8,128)(2,1)S(1)} all-to-all(bf16[4,96,384]{2,1,0:T(8,128)(2,1)} %shard_map.123), channel_id=1, replica_groups=mesh['y'=4,'z'=2,'x'=4,'zlo'=2,'core'=2] {'y'}, dimensions={0} | all-to-all | bytes 589824 | tf_op jit(solution)/shard_map/all_to_all | solution.py:37
  13.3 1.7 broadcast_in_dim.18
  14.9 7.3 %all-to-all-start.1 = ((bf16[8,4,96,384]{3,2,1,0:T(8,128)(2,1)}), bf16[8,4,96,384]{3,2,1,0:T(8,128)(2,1)S(1)}, u32[]{:S(2)}, u32[]{:S(2)}) async-start(bf16[8,4,96,384]{3,2,1,0:T(8,128)(2,1)} %broadcast_in_dim.18), calls=%async_computation.1 | async-start | bytes 4718592 | tf_op jit(solution)/shard_map/all_to_all | solution.py:37
  22.9 4.3 %shard_map.122 = (bf16[128,3072]{1,0:T(8,128)(2,1)}, bf16[128,1536]{1,0:T(8,128)(2,1)}, bf16[128,1536]{1,0:T(8,128)(2,1)}, bf16[128,1536]{1,0:T(8,128)(2,1)}, bf...) custom-call(s32[2]{0:T(128)} %pad_add_fusion.at, ...), custom_call_target="tpu_custom_call" | custom-call | tf_op jit(solution)/shard_map/pallas_call | solution.py:44
  27.4 1.8 collective-permute-start.1
  30.2 7.2 %collective-permute-done.m1 = bf16[128,1536]{1,0:T(8,128)(2,1)S(1)} collective-permute-done((bf16[128,1536]{1,0:T(8,128)(2,1)}, bf16[128,1536]{1,0:T(8,128)(2,1)S(1)}, u32[]{:S(2)}, u32[]{:S(2)}) %collective-permute-start) | collective-permute-done | bytes 393248 | tf_op jit(solution)/shard_map/ppermute | solution.py:33
  37.5 11.1 %collective-permute-start.3 = (bf16[128,1536]{1,0:T(8,128)(2,1)S(1)}, bf16[128,1536]{1,0:T(8,128)(2,1)}, u32[]{:S(2)}, u32[]{:S(2)}) collective-permute-start(bf16[128,1536]{1,0:T(8,128)(2,1)S(1)} %collective-permute-done.m1), channel_id=1, source_target_pairs={{0,1},{1,0},{2,3},{3,2},{4,5},{5,4},{6,7},{7,6},{8,9},{9,8},{10,11... | collective-permute-start | bytes 1179656 | tf_op jit(solution)/shard_map/ppermute | solution.py:33
  51.1 2.5 %all-to-all-done.1.pieces = bf16[8,4,96,384]{3,2,1,0:T(8,128)(2,1)S(1)} async-done(((bf16[8,4,96,384]{3,2,1,0:T(8,128)(2,1)}), bf16[8,4,96,384]{3,2,1,0:T(8,128)(2,1)S(1)}, u32[]{:S(2)}, u32[]{:S(2)}) %all-to-all-start.1) | async-done | bytes 2359328 | tf_op jit(solution)/shard_map/all_to_all | solution.py:37
  55.1 6.4 %shard_map.124 = (bf16[512,128]{1,0:T(8,128)(2,1)}, bf16[512,256]{1,0:T(8,128)(2,1)}, f32[512,256]{1,0:T(8,128)}, bf16[512,128]{1,0:T(8,128)(2,1)}, bf16[512,128...) custom-call(s32[2]{0:T(128)} %pad_add_fusion.at, bf16[128,3072]{1,0:T(8,128)(2,1)} %get-tuple-element.36.own, ...), custom_call_target="tpu_custom_call" | custom-call | tf_op jit(solution)/shard_map/pallas_call | solution.py:44
  65.2 3.9 %collective-permute-done.7 = bf16[512,128]{1,0:T(8,128)(2,1)S(1)} collective-permute-done((bf16[512,128]{1,0:T(8,128)(2,1)}, bf16[512,128]{1,0:T(8,128)(2,1)S(1)}, u32[]{:S(2)}, u32[]{:S(2)}) %collective-permute-start.7) | collective-permute-done | bytes 131104 | tf_op jit(solution)/shard_map/ppermute | solution.py:33
  69.1 2.0 collective-permute-start.6
  72.2 2.7 %collective-permute-done.6.q1 = bf16[512,128]{1,0:T(8,128)(2,1)S(1)} collective-permute-done((bf16[512,128]{1,0:T(8,128)(2,1)}, bf16[512,128]{1,0:T(8,128)(2,1)S(1)}, u32[]{:S(2)}, u32[]{:S(2)}) %collective-permute-start.6) | collective-permute-done | bytes 131104 | tf_op jit(solution)/shard_map/ppermute | solution.py:33
  74.9 4.7 %collective-permute-done.11.kv1 = bf16[512,256]{1,0:T(8,128)(2,1)S(1)} collective-permute-done((bf16[512,256]{1,0:T(8,128)(2,1)}, bf16[512,256]{1,0:T(8,128)(2,1)S(1)}, u32[]{:S(2)}, u32[]{:S(2)}) %collective-permute-start.11) | collective-permute-done | bytes 262176 | tf_op jit(solution)/shard_map/ppermute | solution.py:33
  80.9 7.5 %shard_map.125 = (f32[8,1024]{1,0:T(8,128)}, f32[128,512]{1,0:T(8,128)}, bf16[128,512]{1,0:T(8,128)(2,1)}) custom-call(bf16[512,128]{1,0:T(8,128)(2,1)} %get-tuple-element.40.q0, bf16[512,128]{1,0:T(8,128)(2,1)} %copy-done.9, bf16[512,128]{1,0:T(8,128)(2,1)} %copy-done.5, bf16[512,128]{1,0:T(8,128)(2,1)} %copy-done.10, ...), custom_call_target="tpu_custom_call" | custom-call | tf_op jit(solution)/shard_map/pallas_call | solution.py:44
  88.5 3.0 %collective-permute-start.14 = (f32[8,1024]{1,0:T(8,128)}, f32[8,1024]{1,0:T(8,128)S(1)}, u32[]{:S(2)}, u32[]{:S(2)}) collective-permute-start(f32[8,1024]{1,0:T(8,128)} %get-tuple-element.45.stats), channel_id=1, source_target_pairs={{0,16},{16,0},{1,17},{17,1},{2,18},{18,2},{3,19},{19,3},{4,20},{20... | collective-permute-start | bytes 98312 | tf_op jit(solution)/shard_map/ppermute | solution.py:33
  91.5 1.5 collective-permute-done.14.sent
  93.6 9.0 %shard_map.126 = (f32[512,128]{1,0:T(8,128)}, bf16[512,128]{1,0:T(8,128)(2,1)}, f32[512,256]{1,0:T(8,128)}, bf16[512,256]{1,0:T(8,128)(2,1)}, bf16[512,256]{1,0:T(8,128)(2,1)}, /*index=5*/bf16[512,256]{1,0:T(8,128)(2,1)}) custom-call(bf16[512,128]{1,0:T(8,128)(2,1)} %get-tuple-element.40.q0, bf16[512,128]{1,0:T(8,128)(2,1)} %copy-done.9, ...), custom_call_target="tpu_custom_call" | custom-call | tf_op jit(solution)/shard_map/pallas_call | solution.py:44
  104.0 3.0 %collective-permute-start.15 = (bf16[512,128]{1,0:T(8,128)(2,1)}, bf16[512,128]{1,0:T(8,128)(2,1)S(1)}, u32[]{:S(2)}, u32[]{:S(2)}) collective-permute-start(bf16[512,128]{1,0:T(8,128)(2,1)} %get-tuple-element.47), channel_id=1, source_target_pairs={{0,16},{16,0},{1,17},{17,1},{2,18},{18,2},{3,19},{19,3},{4,20},{20... | collective-permute-start | bytes 393224 | tf_op jit(solution)/shard_map/ppermute | solution.py:33
  107.0 2.6 %collective-permute-done.15.dq1 = bf16[512,128]{1,0:T(8,128)(2,1)S(1)} collective-permute-done((bf16[512,128]{1,0:T(8,128)(2,1)}, bf16[512,128]{1,0:T(8,128)(2,1)S(1)}, u32[]{:S(2)}, u32[]{:S(2)}) %collective-permute-start.15) | collective-permute-done | bytes 131104 | tf_op jit(solution)/shard_map/ppermute | solution.py:33
  109.7 7.4 %collective-permute-done.18.dkv3 = bf16[512,256]{1,0:T(8,128)(2,1)S(1)} collective-permute-done((bf16[512,256]{1,0:T(8,128)(2,1)}, bf16[512,256]{1,0:T(8,128)(2,1)S(1)}, u32[]{:S(2)}, u32[]{:S(2)}) %collective-permute-start.18) | collective-permute-done | bytes 262176 | tf_op jit(solution)/shard_map/ppermute | solution.py:33
  117.8 5.6 %shard_map.127 = (bf16[512,1536]{1,0:T(8,128)(2,1)}, bf16[512,1536]{1,0:T(8,128)(2,1)}) custom-call(s32[2]{0:T(128)} %pad_add_fusion.at, f32[512,128]{1,0:T(8,128)} %get-tuple-element.46.dq0, bf16[512,128]{1,0:T(8,128)(2,1)} %copy-done.27, f32[512,256]{1,0:T(8,128)} %get-tuple-element.48.dkv0, bf16[512,256]{1,0:T(8,128)(2,1)} %copy-done.18, ...), custom_call_target="tpu_custom_call" | custom-call | tf_op jit(solution)/shard_map/pallas_call | solution.py:44
  123.4 1.6 collective-permute-start.19
  125.0 3.2 %collective-permute-done.19.got = bf16[512,1536]{1,0:T(8,128)(2,1)S(1)} collective-permute-done((bf16[512,1536]{1,0:T(8,128)(2,1)}, bf16[512,1536]{1,0:T(8,128)(2,1)S(1)}, u32[]{:S(2)}, u32[]{:S(2)}) %collective-permute-start.19) | collective-permute-done | bytes 1572896 | tf_op jit(solution)/shard_map/ppermute | solution.py:33
  129.5 3.2 %shard_map.128 = (bf16[128,1536]{1,0:T(8,128)(2,1)}, bf16[128,1536]{1,0:T(8,128)(2,1)}, bf16[128,1536]{1,0:T(8,128)(2,1)}, bf16[128,1536]{1,0:T(8,128)(2,1)}) custom-call(bf16[512,1536]{1,0:T(8,128)(2,1)} %get-tuple-element.54.kept, bf16[512,1536]{1,0:T(8,128)(2,1)} %copy-done.2), custom_call_target="tpu_custom_call" | custom-call | tf_op jit(solution)/shard_map/pallas_call | solution.py:44
  132.7 7.2 %collective-permute-start.20 = (bf16[128,1536]{1,0:T(8,128)(2,1)}, bf16[128,1536]{1,0:T(8,128)(2,1)S(1)}, u32[]{:S(2)}, u32[]{:S(2)}) collective-permute-start(bf16[128,1536]{1,0:T(8,128)(2,1)} %get-tuple-element.57), channel_id=1, source_target_pairs={{0,96},{32,0},{64,32},{1,97},{33,1},{65,33},{2,98},{34,2},{66,34},... | collective-permute-start | bytes 1179656 | tf_op jit(solution)/shard_map/ppermute | solution.py:33
  139.8 1.9 collective-permute-start.21
  141.7 1.9 collective-permute-start.22
  143.6 13.0 %collective-permute-done.20.p1 = bf16[128,1536]{1,0:T(8,128)(2,1)S(1)} collective-permute-done((bf16[128,1536]{1,0:T(8,128)(2,1)}, bf16[128,1536]{1,0:T(8,128)(2,1)S(1)}, u32[]{:S(2)}, u32[]{:S(2)}) %collective-permute-start.20) | collective-permute-done | bytes 393248 | tf_op jit(solution)/shard_map/ppermute | solution.py:33
  156.6 2.0 collective-permute-done.22.p3
  159.4 2.3 %shard_map.129 = bf16[128,1536]{1,0:T(8,128)(2,1)} custom-call(bf16[128,1536]{1,0:T(8,128)(2,1)} %get-tuple-element.56.p0, bf16[128,1536]{1,0:T(8,128)(2,1)} %copy-done.14, bf16[128,1536]{1,0:T(8,128)(2,1)} %copy-done.15, bf16[128,1536]{1,0:T(8,128)(2,1)} %copy-done.16), custom_call_target="tpu_custom_call" | custom-call | tf_op jit(solution)/shard_map/pallas_call | solution.py:44
  162.4 2.1 collective-permute-start.29
  164.5 2.6 %collective-permute-start.30 = (bf16[128,768]{1,0:T(8,128)(2,1)S(1)}, bf16[128,768]{1,0:T(8,128)(2,1)S(1)}, u32[]{:S(2)}, u32[]{:S(2)}) collective-permute-start(bf16[128,768]{1,0:T(8,128)(2,1)S(1)} %copy-done.31), channel_id=1, source_target_pairs={{0,64},{32,96},{64,0},{96,32},{1,65},{33,97},{65,1},{97,33},{2,66}... | collective-permute-start | bytes 589832 | tf_op jit(solution)/shard_map/ppermute | solution.py:33
  167.1 2.9 %collective-permute-start.25 = (bf16[128,512]{1,0:T(8,128)(2,1)S(1)}, bf16[128,512]{1,0:T(8,128)(2,1)S(1)}, u32[]{:S(2)}, u32[]{:S(2)}) collective-permute-start(bf16[128,512]{1,0:T(8,128)(2,1)S(1)} %copy-done.33), channel_id=1, source_target_pairs={{0,16},{16,0},{1,17},{17,1},{2,18},{18,2},{3,19},{19,3},{4,20},{20... | collective-permute-start | bytes 393224 | tf_op jit(solution)/shard_map/ppermute | solution.py:33
  170.0 1.6 collective-permute-start.31
  171.6 4.6 %collective-permute-done.25.other = bf16[128,512]{1,0:T(8,128)(2,1)S(1)} collective-permute-done((bf16[128,512]{1,0:T(8,128)(2,1)S(1)}, bf16[128,512]{1,0:T(8,128)(2,1)S(1)}, u32[]{:S(2)}, u32[]{:S(2)}) %collective-permute-start.25) | collective-permute-done | bytes 131104 | tf_op jit(solution)/shard_map/ppermute | solution.py:33
  176.9 1.9 shard_map.131
  178.9 3.7 %collective-permute-start.26 = (bf16[512,128]{1,0:T(8,128)(2,1)}, bf16[512,128]{1,0:T(8,128)(2,1)S(1)}, u32[]{:S(2)}, u32[]{:S(2)}) collective-permute-start(bf16[512,128]{1,0:T(8,128)(2,1)} %get-tuple-element.63), channel_id=1, source_target_pairs={{0,32},{32,64},{64,96},{1,33},{33,65},{65,97},{2,34},{34,66},{66,9... | collective-permute-start | bytes 393224 | tf_op jit(solution)/shard_map/ppermute | solution.py:33
  182.6 5.1 %collective-permute-start.27 = (bf16[512,128]{1,0:T(8,128)(2,1)}, bf16[512,128]{1,0:T(8,128)(2,1)S(1)}, u32[]{:S(2)}, u32[]{:S(2)}) collective-permute-start(bf16[512,128]{1,0:T(8,128)(2,1)} %get-tuple-element.64), channel_id=1, source_target_pairs={{0,64},{32,96},{64,0},{1,65},{33,97},{65,1},{2,66},{34,98},{66,2},... | collective-permute-start | bytes 393224 | tf_op jit(solution)/shard_map/ppermute | solution.py:33
  187.8 1.9 collective-permute-start.28
  189.7 1.7 collective-permute-done.27.m2
  191.4 2.3 %collective-permute-done.28.m3 = bf16[512,128]{1,0:T(8,128)(2,1)S(1)} collective-permute-done((bf16[512,128]{1,0:T(8,128)(2,1)}, bf16[512,128]{1,0:T(8,128)(2,1)S(1)}, u32[]{:S(2)}, u32[]{:S(2)}) %collective-permute-start.28) | collective-permute-done | bytes 131104 | tf_op jit(solution)/shard_map/ppermute | solution.py:33
  194.3 2.9 %shard_map.132 = bf16[8,96,384]{2,1,0:T(8,128)(2,1)} custom-call(s32[2]{0:T(128)} %pad_add_fusion.at, bf16[512,128]{1,0:T(8,128)(2,1)} %get-tuple-element.62.m0, bf16[512,128]{1,0:T(8,128)(2,1)} %copy-done.25, bf16[512,128]{1,0:T(8,128)(2,1)} %copy-done.26, bf16[512,128]{1,0:T(8,128)(2,1)} %copy-done.28, bf16[128,768]{1,0:T(8,128)(2,1)} %get-tuple-element.66.c0, ...), custom_call_target="tpu_custom_call" | custom-call | tf_op jit(solution)/shard_map/pallas_call | solution.py:44
  197.2 3.5 %all-to-all-start.2 = ((bf16[8,96,384]{2,1,0:T(8,128)(2,1)}), bf16[8,96,384]{2,1,0:T(8,128)(2,1)S(1)}, u32[]{:S(2)}, u32[]{:S(2)}) async-start(bf16[8,96,384]{2,1,0:T(8,128)(2,1)} %shard_map.132), calls=%async_computation.2 | async-start | bytes 1179648 | tf_op jit(solution)/shard_map/all_to_all | solution.py:37
  200.9 3.6 %collective-permute-start.24 = (bf16[128,1536]{1,0:T(8,128)(2,1)S(1)}, bf16[128,1536]{1,0:T(8,128)(2,1)S(1)}, u32[]{:S(2)}, u32[]{:S(2)}) collective-permute-start(bf16[128,1536]{1,0:T(8,128)(2,1)S(1)} %add_convert_fusion.mine), channel_id=1, source_target_pairs={{0,1},{1,0},{2,3},{3,2},{4,5},{5,4},{6,7},{7,6},{8,9},{9,8},{10,11... | collective-permute-start | bytes 1179656 | tf_op jit(solution)/shard_map/ppermute | solution.py:33
  204.4 5.6 %all-to-all-done.2.parts = bf16[8,96,384]{2,1,0:T(8,128)(2,1)S(1)} async-done(((bf16[8,96,384]{2,1,0:T(8,128)(2,1)}), bf16[8,96,384]{2,1,0:T(8,128)(2,1)S(1)}, u32[]{:S(2)}, u32[]{:S(2)}) %all-to-all-start.2) | async-done | bytes 589856 | tf_op jit(solution)/shard_map/all_to_all | solution.py:37
  210.9 1.8 shard_map.133
  213.4 3.3 %shard_map.130 = bf16[128,3072]{1,0:T(8,128)(2,1)} custom-call(s32[2]{0:T(128)} %pad_add_fusion.at, bf16[128,3072]{1,0:T(8,128)(2,1)} %hidden.3, bf16[128,1536]{1,0:T(8,128)(2,1)} %copy-done.4, bf16[128,1536]{1,0:T(8,128)(2,1)} %copy-done.17, f32[1,3072]{1,0:T(1,128)} %bitcast.10), custom_call_target="tpu_custom_call" | custom-call | tf_op jit(solution)/shard_map/pallas_call | solution.py:44
  (107 shorter events, 20.5 us)
Async XLA Ops:
  14.9 38.7 %all-to-all-start.1 = ((bf16[8,4,96,384]{3,2,1,0:T(8,128)(2,1)}), bf16[8,4,96,384]{3,2,1,0:T(8,128)(2,1)S(1)}, u32[]{:S(2)}, u32[]{:S(2)}) async-start(bf16[8,4,96,384]{3,2,1,0:T(8,128)(2,1)} %broadcast_in_dim.18), calls=%async_computation.1 | async-start | bytes 4718592 | tf_op jit(solution)/shard_map/all_to_all | solution.py:37
  27.1 10.3 %collective-permute-start = (bf16[128,1536]{1,0:T(8,128)(2,1)}, bf16[128,1536]{1,0:T(8,128)(2,1)S(1)}, u32[]{:S(2)}, u32[]{:S(2)}) collective-permute-start(bf16[128,1536]{1,0:T(8,128)(2,1)} %get-tuple-element.37), channel_id=1, source_target_pairs={{0,32},{32,64},{64,96},{96,0},{1,33},{33,65},{65,97},{97,1},{2,34}... | collective-permute-start | bytes 1179656 | tf_op jit(solution)/shard_map/ppermute | solution.py:33
  27.4 21.1 %collective-permute-start.1 = (bf16[128,1536]{1,0:T(8,128)(2,1)}, bf16[128,1536]{1,0:T(8,128)(2,1)S(1)}, u32[]{:S(2)}, u32[]{:S(2)}) collective-permute-start(bf16[128,1536]{1,0:T(8,128)(2,1)} %get-tuple-element.38), channel_id=1, source_target_pairs={{0,64},{32,96},{64,0},{96,32},{1,65},{33,97},{65,1},{97,33},{2,66}... | collective-permute-start | bytes 1179656 | tf_op jit(solution)/shard_map/ppermute | solution.py:33
  29.2 19.4 %collective-permute-start.2 = (bf16[128,1536]{1,0:T(8,128)(2,1)}, bf16[128,1536]{1,0:T(8,128)(2,1)S(1)}, u32[]{:S(2)}, u32[]{:S(2)}) collective-permute-start(bf16[128,1536]{1,0:T(8,128)(2,1)} %get-tuple-element.39), channel_id=1, source_target_pairs={{0,96},{32,0},{64,32},{96,64},{1,97},{33,1},{65,33},{97,65},{2,98}... | collective-permute-start | bytes 1179656 | tf_op jit(solution)/shard_map/ppermute | solution.py:33
  37.5 16.2 %copy-start.11 = (bf16[128,1536]{1,0:T(8,128)(2,1)}, bf16[128,1536]{1,0:T(8,128)(2,1)S(1)}, u32[]{:S(2)}) copy-start(bf16[128,1536]{1,0:T(8,128)(2,1)S(1)} %collective-permute-done.m1) | copy-start | bytes 1179652
  37.5 13.0 %collective-permute-start.3 = (bf16[128,1536]{1,0:T(8,128)(2,1)S(1)}, bf16[128,1536]{1,0:T(8,128)(2,1)}, u32[]{:S(2)}, u32[]{:S(2)}) collective-permute-start(bf16[128,1536]{1,0:T(8,128)(2,1)S(1)} %collective-permute-done.m1), channel_id=1, source_target_pairs={{0,1},{1,0},{2,3},{3,2},{4,5},{5,4},{6,7},{7,6},{8,9},{9,8},{10,11... | collective-permute-start | bytes 1179656 | tf_op jit(solution)/shard_map/ppermute | solution.py:33
  48.5 5.1 %copy-start.12 = (bf16[128,1536]{1,0:T(8,128)(2,1)}, bf16[128,1536]{1,0:T(8,128)(2,1)S(1)}, u32[]{:S(2)}) copy-start(bf16[128,1536]{1,0:T(8,128)(2,1)S(1)} %collective-permute-done.1.m2) | copy-start | bytes 1179652
  48.5 2.0 collective-permute-start.4
  48.6 2.5 %collective-permute-start.5 = (bf16[128,1536]{1,0:T(8,128)(2,1)S(1)}, bf16[128,1536]{1,0:T(8,128)(2,1)}, u32[]{:S(2)}, u32[]{:S(2)}) collective-permute-start(bf16[128,1536]{1,0:T(8,128)(2,1)S(1)} %collective-permute-done.2.m3), channel_id=1, source_target_pairs={{0,1},{1,0},{2,3},{3,2},{4,5},{5,4},{6,7},{7,6},{8,9},{9,8},{10,11... | collective-permute-start | bytes 1179656 | tf_op jit(solution)/shard_map/ppermute | solution.py:33
  61.5 7.6 %collective-permute-start.7 = (bf16[512,128]{1,0:T(8,128)(2,1)}, bf16[512,128]{1,0:T(8,128)(2,1)S(1)}, u32[]{:S(2)}, u32[]{:S(2)}) collective-permute-start(bf16[512,128]{1,0:T(8,128)(2,1)} %get-tuple-element.41), channel_id=1, source_target_pairs={{96,0},{97,1},{98,2},{99,3},{100,4},{101,5},{102,6},{103,7},{104,8... | collective-permute-start | bytes 393224 | tf_op jit(solution)/shard_map/ppermute | solution.py:33
  62.8 6.3 %collective-permute-start.8 = (bf16[512,128]{1,0:T(8,128)(2,1)}, bf16[512,128]{1,0:T(8,128)(2,1)S(1)}, u32[]{:S(2)}, u32[]{:S(2)}) collective-permute-start(bf16[512,128]{1,0:T(8,128)(2,1)} %get-tuple-element.42), channel_id=1, source_target_pairs={{96,32},{97,33},{98,34},{99,35},{100,36},{101,37},{102,38},{103,39... | collective-permute-start | bytes 393224 | tf_op jit(solution)/shard_map/ppermute | solution.py:33
  63.4 7.6 %collective-permute-start.9 = (bf16[512,128]{1,0:T(8,128)(2,1)}, bf16[512,128]{1,0:T(8,128)(2,1)S(1)}, u32[]{:S(2)}, u32[]{:S(2)}) collective-permute-start(bf16[512,128]{1,0:T(8,128)(2,1)} %get-tuple-element.43), channel_id=1, source_target_pairs={{96,64},{97,65},{98,66},{99,67},{100,68},{101,69},{102,70},{103,71... | collective-permute-start | bytes 393224 | tf_op jit(solution)/shard_map/ppermute | solution.py:33
  64.1 10.8 %collective-permute-start.13 = (bf16[512,256]{1,0:T(8,128)(2,1)}, bf16[512,256]{1,0:T(8,128)(2,1)S(1)}, u32[]{:S(2)}, u32[]{:S(2)}) collective-permute-start(bf16[512,256]{1,0:T(8,128)(2,1)} %get-tuple-element.44.kv0), channel_id=1, source_target_pairs={{0,12},{4,0},{8,4},{12,8},{1,13},{5,1},{9,5},{13,9},{2,14},{6,2},{... | collective-permute-start | bytes 786440 | tf_op jit(solution)/shard_map/ppermute | solution.py:33
  64.8 10.1 %collective-permute-start.12 = (bf16[512,256]{1,0:T(8,128)(2,1)}, bf16[512,256]{1,0:T(8,128)(2,1)S(1)}, u32[]{:S(2)}, u32[]{:S(2)}) collective-permute-start(bf16[512,256]{1,0:T(8,128)(2,1)} %get-tuple-element.44.kv0), channel_id=1, source_target_pairs={{0,8},{4,12},{8,0},{12,4},{1,9},{5,13},{9,1},{13,5},{2,10},{6,14},... | collective-permute-start | bytes 786440 | tf_op jit(solution)/shard_map/ppermute | solution.py:33
  69.1 10.5 %collective-permute-start.11 = (bf16[512,256]{1,0:T(8,128)(2,1)}, bf16[512,256]{1,0:T(8,128)(2,1)S(1)}, u32[]{:S(2)}, u32[]{:S(2)}) collective-permute-start(bf16[512,256]{1,0:T(8,128)(2,1)} %get-tuple-element.44.kv0), channel_id=1, source_target_pairs={{0,4},{4,8},{8,12},{12,0},{1,5},{5,9},{9,13},{13,1},{2,6},{6,10},{... | collective-permute-start | bytes 786440 | tf_op jit(solution)/shard_map/ppermute | solution.py:33
  69.1 5.8 %collective-permute-start.6 = (bf16[512,128]{1,0:T(8,128)(2,1)}, bf16[512,128]{1,0:T(8,128)(2,1)S(1)}, u32[]{:S(2)}, u32[]{:S(2)}) collective-permute-start(bf16[512,128]{1,0:T(8,128)(2,1)} %get-tuple-element.40.q0), channel_id=1, source_target_pairs={{0,16},{16,0},{1,17},{17,1},{2,18},{18,2},{3,19},{19,3},{4,20},{20... | collective-permute-start | bytes 393224 | tf_op jit(solution)/shard_map/ppermute | solution.py:33
  71.1 8.5 %copy-start.5 = (bf16[512,128]{1,0:T(8,128)(2,1)}, bf16[512,128]{1,0:T(8,128)(2,1)S(1)}, u32[]{:S(2)}) copy-start(bf16[512,128]{1,0:T(8,128)(2,1)S(1)} %add_add_fusion.g0) | copy-start | bytes 393220
  71.1 8.4 %collective-permute-start.10 = (bf16[512,128]{1,0:T(8,128)(2,1)S(1)}, bf16[512,128]{1,0:T(8,128)(2,1)S(1)}, u32[]{:S(2)}, u32[]{:S(2)}) collective-permute-start(bf16[512,128]{1,0:T(8,128)(2,1)S(1)} %add_add_fusion.g0), channel_id=1, source_target_pairs={{0,16},{16,0},{1,17},{17,1},{2,18},{18,2},{3,19},{19,3},{4,20},{20... | collective-permute-start | bytes 393224 | tf_op jit(solution)/shard_map/ppermute | solution.py:33
  88.5 4.5 %collective-permute-start.14 = (f32[8,1024]{1,0:T(8,128)}, f32[8,1024]{1,0:T(8,128)S(1)}, u32[]{:S(2)}, u32[]{:S(2)}) collective-permute-start(f32[8,1024]{1,0:T(8,128)} %get-tuple-element.45.stats), channel_id=1, source_target_pairs={{0,16},{16,0},{1,17},{17,1},{2,18},{18,2},{3,19},{19,3},{4,20},{20... | collective-permute-start | bytes 98312 | tf_op jit(solution)/shard_map/ppermute | solution.py:33
  102.5 7.0 %collective-permute-start.16 = (bf16[512,256]{1,0:T(8,128)(2,1)}, bf16[512,256]{1,0:T(8,128)(2,1)S(1)}, u32[]{:S(2)}, u32[]{:S(2)}) collective-permute-start(bf16[512,256]{1,0:T(8,128)(2,1)} %get-tuple-element.49), channel_id=1, source_target_pairs={{0,12},{4,0},{8,4},{12,8},{1,13},{5,1},{9,5},{13,9},{2,14},{6,2},{... | collective-permute-start | bytes 786440 | tf_op jit(solution)/shard_map/ppermute | solution.py:33
  102.5 7.1 %collective-permute-start.17 = (bf16[512,256]{1,0:T(8,128)(2,1)}, bf16[512,256]{1,0:T(8,128)(2,1)S(1)}, u32[]{:S(2)}, u32[]{:S(2)}) collective-permute-start(bf16[512,256]{1,0:T(8,128)(2,1)} %get-tuple-element.50), channel_id=1, source_target_pairs={{0,8},{4,12},{8,0},{12,4},{1,9},{5,13},{9,1},{13,5},{2,10},{6,14},... | collective-permute-start | bytes 786440 | tf_op jit(solution)/shard_map/ppermute | solution.py:33
  103.4 13.6 %collective-permute-start.18 = (bf16[512,256]{1,0:T(8,128)(2,1)}, bf16[512,256]{1,0:T(8,128)(2,1)S(1)}, u32[]{:S(2)}, u32[]{:S(2)}) collective-permute-start(bf16[512,256]{1,0:T(8,128)(2,1)} %get-tuple-element.51), channel_id=1, source_target_pairs={{0,4},{4,8},{8,12},{12,0},{1,5},{5,9},{9,13},{13,1},{2,6},{6,10},{... | collective-permute-start | bytes 786440 | tf_op jit(solution)/shard_map/ppermute | solution.py:33
  104.0 5.5 %collective-permute-start.15 = (bf16[512,128]{1,0:T(8,128)(2,1)}, bf16[512,128]{1,0:T(8,128)(2,1)S(1)}, u32[]{:S(2)}, u32[]{:S(2)}) collective-permute-start(bf16[512,128]{1,0:T(8,128)(2,1)} %get-tuple-element.47), channel_id=1, source_target_pairs={{0,16},{16,0},{1,17},{17,1},{2,18},{18,2},{3,19},{19,3},{4,20},{20... | collective-permute-start | bytes 393224 | tf_op jit(solution)/shard_map/ppermute | solution.py:33
  109.5 7.5 %copy-start.27 = (bf16[512,128]{1,0:T(8,128)(2,1)}, bf16[512,128]{1,0:T(8,128)(2,1)S(1)}, u32[]{:S(2)}) copy-start(bf16[512,128]{1,0:T(8,128)(2,1)S(1)} %collective-permute-done.15.dq1) | copy-start | bytes 393220
  109.6 7.5 %copy-start.18 = (bf16[512,256]{1,0:T(8,128)(2,1)}, bf16[512,256]{1,0:T(8,128)(2,1)S(1)}, u32[]{:S(2)}) copy-start(bf16[512,256]{1,0:T(8,128)(2,1)S(1)} %collective-permute-done.16.dkv1) | copy-start | bytes 786436
  109.7 7.4 %copy-start.19 = (bf16[512,256]{1,0:T(8,128)(2,1)}, bf16[512,256]{1,0:T(8,128)(2,1)S(1)}, u32[]{:S(2)}) copy-start(bf16[512,256]{1,0:T(8,128)(2,1)S(1)} %collective-permute-done.17.dkv2) | copy-start | bytes 786436
  123.4 4.8 %collective-permute-start.19 = (bf16[512,1536]{1,0:T(8,128)(2,1)}, bf16[512,1536]{1,0:T(8,128)(2,1)S(1)}, u32[]{:S(2)}, u32[]{:S(2)}) collective-permute-start(bf16[512,1536]{1,0:T(8,128)(2,1)} %get-tuple-element.55), channel_id=1, source_target_pairs={{0,1},{1,0},{2,3},{3,2},{4,5},{5,4},{6,7},{7,6},{8,9},{9,8},{10,11... | collective-permute-start | bytes 4718600 | tf_op jit(solution)/shard_map/ppermute | solution.py:33
  129.5 33.0 %copy-start.32 = (bf16[128,768]{1,0:T(8,128)(2,1)S(1)}, bf16[128,768]{1,0:T(8,128)(2,1)}, u32[]{:S(2)}) copy-start(bf16[128,768]{1,0:T(8,128)(2,1)} %get-tuple-element.67) | copy-start | bytes 589828
  129.5 35.0 %copy-start.31 = (bf16[128,768]{1,0:T(8,128)(2,1)S(1)}, bf16[128,768]{1,0:T(8,128)(2,1)}, u32[]{:S(2)}) copy-start(bf16[128,768]{1,0:T(8,128)(2,1)} %get-tuple-element.68) | copy-start | bytes 589828
  129.5 37.7 %copy-start.33 = (bf16[128,512]{1,0:T(8,128)(2,1)S(1)}, bf16[128,512]{1,0:T(8,128)(2,1)}, u32[]{:S(2)}) copy-start(bf16[128,512]{1,0:T(8,128)(2,1)} %get-tuple-element.61) | copy-start | bytes 393220
  129.5 40.5 %copy-start.30 = (bf16[128,768]{1,0:T(8,128)(2,1)S(1)}, bf16[128,768]{1,0:T(8,128)(2,1)}, u32[]{:S(2)}) copy-start(bf16[128,768]{1,0:T(8,128)(2,1)} %get-tuple-element.69) | copy-start | bytes 589828
  132.7 24.0 %collective-permute-start.20 = (bf16[128,1536]{1,0:T(8,128)(2,1)}, bf16[128,1536]{1,0:T(8,128)(2,1)S(1)}, u32[]{:S(2)}, u32[]{:S(2)}) collective-permute-start(bf16[128,1536]{1,0:T(8,128)(2,1)} %get-tuple-element.57), channel_id=1, source_target_pairs={{0,96},{32,0},{64,32},{1,97},{33,1},{65,33},{2,98},{34,2},{66,34},... | collective-permute-start | bytes 1179656 | tf_op jit(solution)/shard_map/ppermute | solution.py:33
  139.8 16.8 %collective-permute-start.21 = (bf16[128,1536]{1,0:T(8,128)(2,1)}, bf16[128,1536]{1,0:T(8,128)(2,1)S(1)}, u32[]{:S(2)}, u32[]{:S(2)}) collective-permute-start(bf16[128,1536]{1,0:T(8,128)(2,1)} %get-tuple-element.58), channel_id=1, source_target_pairs={{0,64},{32,96},{64,0},{1,65},{33,97},{65,1},{2,66},{34,98},{66,2},... | collective-permute-start | bytes 1179656 | tf_op jit(solution)/shard_map/ppermute | solution.py:33
  141.7 16.9 %collective-permute-start.22 = (bf16[128,1536]{1,0:T(8,128)(2,1)}, bf16[128,1536]{1,0:T(8,128)(2,1)S(1)}, u32[]{:S(2)}, u32[]{:S(2)}) collective-permute-start(bf16[128,1536]{1,0:T(8,128)(2,1)} %get-tuple-element.59), channel_id=1, source_target_pairs={{0,32},{32,64},{64,96},{1,33},{33,65},{65,97},{2,34},{34,66},{66,9... | collective-permute-start | bytes 1179656 | tf_op jit(solution)/shard_map/ppermute | solution.py:33
  161.7 39.1 %copy-start.3 = (bf16[128,1536]{1,0:T(8,128)(2,1)S(1)}, bf16[128,1536]{1,0:T(8,128)(2,1)}, u32[]{:S(2)}) copy-start(bf16[128,1536]{1,0:T(8,128)(2,1)} %shard_map.129) | copy-start | bytes 1179652
  161.7 39.1 %collective-permute-start.23 = (bf16[128,1536]{1,0:T(8,128)(2,1)}, bf16[128,1536]{1,0:T(8,128)(2,1)S(1)}, u32[]{:S(2)}, u32[]{:S(2)}) collective-permute-start(bf16[128,1536]{1,0:T(8,128)(2,1)} %shard_map.129), channel_id=1, source_target_pairs={{0,2},{2,0},{1,3},{3,1},{4,6},{6,4},{5,7},{7,5},{8,10},{10,8},{9,1... | collective-permute-start | bytes 1179656 | tf_op jit(solution)/shard_map/ppermute | solution.py:33
  162.4 20.2 %collective-permute-start.29 = (bf16[128,768]{1,0:T(8,128)(2,1)S(1)}, bf16[128,768]{1,0:T(8,128)(2,1)S(1)}, u32[]{:S(2)}, u32[]{:S(2)}) collective-permute-start(bf16[128,768]{1,0:T(8,128)(2,1)S(1)} %copy-done.32), channel_id=1, source_target_pairs={{0,32},{32,64},{64,96},{96,0},{1,33},{33,65},{65,97},{97,1},{2,34}... | collective-permute-start | bytes 589832 | tf_op jit(solution)/shard_map/ppermute | solution.py:33
  164.5 23.2 %collective-permute-start.30 = (bf16[128,768]{1,0:T(8,128)(2,1)S(1)}, bf16[128,768]{1,0:T(8,128)(2,1)S(1)}, u32[]{:S(2)}, u32[]{:S(2)}) collective-permute-start(bf16[128,768]{1,0:T(8,128)(2,1)S(1)} %copy-done.31), channel_id=1, source_target_pairs={{0,64},{32,96},{64,0},{96,32},{1,65},{33,97},{65,1},{97,33},{2,66}... | collective-permute-start | bytes 589832 | tf_op jit(solution)/shard_map/ppermute | solution.py:33
  167.1 9.1 %collective-permute-start.25 = (bf16[128,512]{1,0:T(8,128)(2,1)S(1)}, bf16[128,512]{1,0:T(8,128)(2,1)S(1)}, u32[]{:S(2)}, u32[]{:S(2)}) collective-permute-start(bf16[128,512]{1,0:T(8,128)(2,1)S(1)} %copy-done.33), channel_id=1, source_target_pairs={{0,16},{16,0},{1,17},{17,1},{2,18},{18,2},{3,19},{19,3},{4,20},{20... | collective-permute-start | bytes 393224 | tf_op jit(solution)/shard_map/ppermute | solution.py:33
  170.0 19.7 %collective-permute-start.31 = (bf16[128,768]{1,0:T(8,128)(2,1)S(1)}, bf16[128,768]{1,0:T(8,128)(2,1)S(1)}, u32[]{:S(2)}, u32[]{:S(2)}) collective-permute-start(bf16[128,768]{1,0:T(8,128)(2,1)S(1)} %copy-done.30), channel_id=1, source_target_pairs={{0,96},{32,0},{64,32},{96,64},{1,97},{33,1},{65,33},{97,65},{2,98}... | collective-permute-start | bytes 589832 | tf_op jit(solution)/shard_map/ppermute | solution.py:33
  178.9 10.9 %collective-permute-start.26 = (bf16[512,128]{1,0:T(8,128)(2,1)}, bf16[512,128]{1,0:T(8,128)(2,1)S(1)}, u32[]{:S(2)}, u32[]{:S(2)}) collective-permute-start(bf16[512,128]{1,0:T(8,128)(2,1)} %get-tuple-element.63), channel_id=1, source_target_pairs={{0,32},{32,64},{64,96},{1,33},{33,65},{65,97},{2,34},{34,66},{66,9... | collective-permute-start | bytes 393224 | tf_op jit(solution)/shard_map/ppermute | solution.py:33
  182.6 11.1 %copy-start.21 = (bf16[128,768]{1,0:T(8,128)(2,1)}, bf16[128,768]{1,0:T(8,128)(2,1)S(1)}, u32[]{:S(2)}) copy-start(bf16[128,768]{1,0:T(8,128)(2,1)S(1)} %collective-permute-done.29.c1) | copy-start | bytes 589828
  182.6 8.8 %collective-permute-start.27 = (bf16[512,128]{1,0:T(8,128)(2,1)}, bf16[512,128]{1,0:T(8,128)(2,1)S(1)}, u32[]{:S(2)}, u32[]{:S(2)}) collective-permute-start(bf16[512,128]{1,0:T(8,128)(2,1)} %get-tuple-element.64), channel_id=1, source_target_pairs={{0,64},{32,96},{64,0},{1,65},{33,97},{65,1},{2,66},{34,98},{66,2},... | collective-permute-start | bytes 393224 | tf_op jit(solution)/shard_map/ppermute | solution.py:33
  187.8 5.9 %copy-start.22 = (bf16[128,768]{1,0:T(8,128)(2,1)}, bf16[128,768]{1,0:T(8,128)(2,1)S(1)}, u32[]{:S(2)}) copy-start(bf16[128,768]{1,0:T(8,128)(2,1)S(1)} %collective-permute-done.30.c2) | copy-start | bytes 589828
  187.8 5.9 %collective-permute-start.28 = (bf16[512,128]{1,0:T(8,128)(2,1)}, bf16[512,128]{1,0:T(8,128)(2,1)S(1)}, u32[]{:S(2)}, u32[]{:S(2)}) collective-permute-start(bf16[512,128]{1,0:T(8,128)(2,1)} %get-tuple-element.65), channel_id=1, source_target_pairs={{0,96},{32,0},{64,32},{1,97},{33,1},{65,33},{2,98},{34,2},{66,34},... | collective-permute-start | bytes 393224 | tf_op jit(solution)/shard_map/ppermute | solution.py:33
  197.2 12.9 %all-to-all-start.2 = ((bf16[8,96,384]{2,1,0:T(8,128)(2,1)}), bf16[8,96,384]{2,1,0:T(8,128)(2,1)S(1)}, u32[]{:S(2)}, u32[]{:S(2)}) async-start(bf16[8,96,384]{2,1,0:T(8,128)(2,1)} %shard_map.132), calls=%async_computation.2 | async-start | bytes 1179648 | tf_op jit(solution)/shard_map/all_to_all | solution.py:37
  200.9 11.8 %copy-start.4 = (bf16[128,1536]{1,0:T(8,128)(2,1)}, bf16[128,1536]{1,0:T(8,128)(2,1)S(1)}, u32[]{:S(2)}) copy-start(bf16[128,1536]{1,0:T(8,128)(2,1)S(1)} %add_convert_fusion.mine) | copy-start | bytes 1179652
  200.9 11.8 %collective-permute-start.24 = (bf16[128,1536]{1,0:T(8,128)(2,1)S(1)}, bf16[128,1536]{1,0:T(8,128)(2,1)S(1)}, u32[]{:S(2)}, u32[]{:S(2)}) collective-permute-start(bf16[128,1536]{1,0:T(8,128)(2,1)S(1)} %add_convert_fusion.mine), channel_id=1, source_target_pairs={{0,1},{1,0},{2,3},{3,2},{4,5},{5,4},{6,7},{7,6},{8,9},{9,8},{10,11... | collective-permute-start | bytes 1179656 | tf_op jit(solution)/shard_map/ppermute | solution.py:33
  (20 other events, 42.2 us)
where the time goes:
time: 221 us; the launch traced here: 217 us
  starting transfers between devices  76.6 us (35%)
  waiting for transfers between devices  65.8 us (30%)
  Pallas kernels  50 us (23%)
  local copies, waits for them, and re-layouts  11.3 us (5%)
  blocking collectives  10.9 us (5%)
    ppermute x32, starting transfers between devices, shifted(): lax.ppermute(array, axis, [(i, (i + shift) % peers) for i in sources])  65.8 us
    ppermute x32, waiting for transfers between devices, shifted(): lax.ppermute(array, axis, [(i, (i + shift) % peers) for i in sources])  57.6 us
    pallas_call x12, Pallas kernels, run(): pl.pallas_call(kernel, out_shape=tuple((jax.ShapeDtypeStruct(s, t) for s,...  50 us
    all_to_all x2, starting transfers between devices, exchanged(): return lax.all_to_all(array, axes, 0, 0, tiled=True)  10.9 us
    all_to_all x1, blocking collectives, exchanged(): return lax.all_to_all(array, axes, 0, 0, tiled=True)  10.9 us
    unnamed x68, local copies, waits for them, and re-layouts  8.82 us
    all_to_all x2, waiting for transfers between devices, exchanged(): return lax.all_to_all(array, axes, 0, 0, tiled=True)  8.16 us
  transfers between devices with their start and end apart: 34, of which 18 were waited for; matrix products, arithmetic and copies ran while one was open for 1% of the time, Pallas kernels for 5%

commit v1 on v0

--- a/solution.py
+++ b/solution.py
@@ -15,8 +15,12 @@
 ROLES = 4
 GRAD_ROLE = 3
 TILE = 256
+UNROLL = 2
 F32 = jnp.float32
 BF16 = jnp.bfloat16
+
+
+PLANE_ORDER = ((0, 1), (1, 0), (0, 3), (1, 1), (1, 3), (0, 2), (1, 2))
 
 
 def nt(a, b):
@@ -57,31 +61,41 @@
     return pl.multiple_of(core * half, half)
 
 
-def pack_kernel(query, key, value, output, packed):
-    for h in range(GRAD_ROLE):
-        at = slice(h * HEAD_DIM, (h + 1) * HEAD_DIM)
-        for n, source in enumerate((query, key, value)):
-            packed[h, :, n * HEAD_DIM : (n + 1) * HEAD_DIM] = source[:, at]
-    packed[GRAD_ROLE] = output[...]
-
-
-def norm_kernel(at, hidden, cot, scale, shift, gate, own, s1, s2, s3, c0, c1, c2, c3):
+def pack_kernel(at, query, key, value, output, own, s1, s2, s3):
+    for j, out in enumerate((own, s1, s2, s3)):
+        role = lax.rem(at[0] + j, ROLES)
+        for h in range(GRAD_ROLE):
+
+            @pl.when(role == h)
+            def _():
+                for n, source in enumerate((query, key, value)):
+                    here = slice(h * HEAD_DIM, (h + 1) * HEAD_DIM)
+                    out[:, n * HEAD_DIM : (n + 1) * HEAD_DIM] = source[:, here]
+
+        @pl.when(role == GRAD_ROLE)
+        def _():
+            out[...] = output[...]
+
+
+def norm_kernel(at, hidden, cot, scale, shift, gate, own, s1, s2, s3, branch, branch_half):
     y, core = at[0], at[1]
     values = hidden[...].astype(F32)
     center = values - jnp.mean(values, axis=-1, keepdims=True)
     inverse = lax.rsqrt(jnp.mean(center * center, axis=-1, keepdims=True) + EPSILON)
     normed = (center * inverse * (1.0 + scale[...]) + shift[...]).astype(BF16)
     graded = (cot[...].astype(F32) * gate[...]).astype(BF16)
-    quarter = c0.shape[1]
-    for n in range(ROLES):
-        for j, part in enumerate((c0, c1, c2, c3)):
-
-            @pl.when(lax.rem(y + j, ROLES) == n)
-            def _():
-                part[...] = graded[:, n * quarter : (n + 1) * quarter]
-
+    branch[...] = graded
     own[...] = jnp.where(y == GRAD_ROLE, graded, normed)
     half = s1.shape[1]
+
+    @pl.when(core == 0)
+    def _():
+        branch_half[...] = graded[:, :half]
+
+    @pl.when(core == 1)
+    def _():
+        branch_half[...] = graded[:, half:]
+
     for j, sent in ((1, s1), (2, s2), (3, s3)):
         wanted = lax.rem(y + j, ROLES) == GRAD_ROLE
 
@@ -95,19 +109,23 @@
 
 
 def project_kernel(
-    at, own, m1, m2, m3, o1, o2, o3, pieces, gains, q_out, kv_out, raw_out, g0, g1, g2, weight
+    at, own, m1, m2, m3, o1, o2, o3, w0, w1, w2, w3, w4, w5, w6, w7, gains,
+    q_out, kv_out, raw_out, g0, g1, g2, w_here, w_there,
 ):
-    y, core = at[0], at[1]
-    groups, _, block, _ = pieces.shape
-    for n in range(groups):
-        for k in range(ROLES):
-            at_row = (k * groups + n) * block
-            weight[at_row : at_row + block, :] = pieces[n, k]
+    y, core, plane = at[0], at[1], at[2]
+    pieces = (w0, w1, w2, w3, w4, w5, w6, w7)
+    block = w0.shape[1]
+    for (dz, dx), piece in zip(((0, 0), *PLANE_ORDER), pieces):
+        source = 4 * lax.rem(plane // 4 + dz, 2) + lax.rem(plane + 4 - dx, 4)
+        for t in range(2):
+            at_row = pl.multiple_of((t * len(pieces) + source) * block, block)
+            w_here[pl.ds(at_row, block), :] = piece[lax.rem(y + ROLES - (2 * core + t), ROLES)]
+            w_there[pl.ds(at_row, block), :] = piece[lax.rem(y + ROLES - (2 - 2 * core + t), ROLES)]
     half = m1.shape[1]
     here, there = half_start(core, half), half_start(1 - core, half)
     mine = jnp.concatenate([own[:, pl.ds(here, half)], m1[...], m2[...], m3[...]], axis=0)
     other = jnp.concatenate([own[:, pl.ds(there, half)], o1[...], o2[...], o3[...]], axis=0)
-    total = nn(mine, weight[pl.ds(here, half), :]) + nn(other, weight[pl.ds(there, half), :])
+    total = nn(mine, w_here[...]) + nn(other, w_there[...])
     plain = y == GRAD_ROLE
     for at_column, gain, factor, out, column in (
         (0, 0, FACTOR, q_out, 0),
@@ -157,7 +175,7 @@
             mixed[:, pl.ds(local, TILE)] = mix_t.astype(mixed.dtype)
             return carry
 
-        lax.fori_loop(0, rows // TILE, step, 0)
+        lax.fori_loop(0, rows // TILE, step, 0, unroll=True)
     stats[3:8, :] = jnp.zeros((5, stats.shape[1]), F32)
 
 
@@ -200,7 +218,7 @@
         query_acc[pl.ds(at, TILE), :] = jnp.transpose(nn(keys_t, score_grad))
         return carry
 
-    lax.fori_loop(0, 2 * rows // TILE, step, 0)
+    lax.fori_loop(0, 2 * rows // TILE, step, 0, unroll=UNROLL)
     dq0[...] = query_acc[:rows, :]
     dq1[...] = query_acc[rows:, :].astype(BF16)
     for n, out in enumerate((dkv0, dkv1, dkv2, dkv3)):
@@ -209,34 +227,29 @@
         out[:, HEAD_DIM:] = value_acc[at, :].astype(out.dtype)
 
 
-def mix_kernel(stats, sent, own, other, m0, m1, m2, m3):
-    rows = own.shape[1]
+def outproj_kernel(at, stats, sent, own, other, branch, c1, c2, c3, d1, d2, d3, out):
+    core = at[1]
+    rows, half = own.shape[1], c1.shape[1]
     _, total, _, a, b = combined(stats[:, :rows], sent[:, rows:])
-    mixed = jnp.transpose((own[...] * a + other[...].astype(F32) * b) / total).astype(BF16)
-    block = rows // ROLES
-    for shift, out in enumerate((m0, m1, m2, m3)):
-        for j in range(ROLES):
-            i = (j - shift) % ROLES
-            out[j * block : (j + 1) * block, :] = mixed[i * block : (i + 1) * block, :]
-
-
-def outproj_kernel(at, m0, m1, m2, m3, c0, c1, c2, c3, out, mixes):
-    y = at[0]
-    for shift, part in enumerate((m0, m1, m2, m3)):
-        head = lax.rem(y + ROLES - shift, ROLES)
-        mixes[:, pl.ds(pl.multiple_of(head * HEAD_DIM, HEAD_DIM), HEAD_DIM)] = part[...]
-    cot = jnp.concatenate([c0[...], c1[...], c2[...], c3[...]], axis=0)
-    total = nn(jnp.transpose(cot), mixes[:, : GRAD_ROLE * HEAD_DIM]).astype(BF16)
-    block = out.shape[1]
-    for n in range(out.shape[0]):
-        out[n] = total[n * block : (n + 1) * block, :]
-
-
-def sum_kernel(parts, out):
-    total = parts[0].astype(F32)
-    for n in range(1, parts.shape[0]):
-        total = total + parts[n].astype(F32)
-    out[...] = total
+    mix_t = ((own[...] * a + other[...].astype(F32) * b) / total).astype(BF16)
+    groups, _, block, _ = out.shape
+    for side, parts in ((core, (c1, c2, c3)), (1 - core, (d1, d2, d3))):
+        first = branch[:, pl.ds(half_start(side, half), half)]
+        cot = jnp.concatenate([first] + [p[...] for p in parts], axis=0)
+        partial = jnp.transpose(nn(mix_t, cot)).astype(BF16)
+        for n in range(groups):
+            for t in range(2):
+                at_row = (t * groups + n) * block
+                out[n, 2 * side + t] = partial[at_row : at_row + block, :]
+
+
+def sum_kernel(at, parts, own, s1, s2, s3):
+    for j, out in enumerate((own, s1, s2, s3)):
+        block = lax.rem(at[0] + ROLES - j, ROLES)
+        total = parts[0, block].astype(F32)
+        for n in range(1, parts.shape[0]):
+            total = total + parts[n, block].astype(F32)
+        out[...] = total
 
 
 def head_back(grad, raw, gain, factor):
@@ -247,26 +260,21 @@
     return (inverse * (scaled - unit * along)).astype(BF16)
 
 
-def back_kernel(at, dq0, dq1, dkv0, dkv1, dkv2, dkv3, raw, gains, weight, kept, sent):
-    y, core = at[0], at[1]
-    half = kept.shape[1]
-    here, there = half_start(core, half), half_start(1 - core, half)
+def back_kernel(at, dq0, dq1, dkv0, dkv1, dkv2, dkv3, raw, gains, grads):
     query_grad = dq0[...] + dq1[...].astype(F32)
     both = dkv0[...] + dkv1[...].astype(F32) + dkv2[...].astype(F32) + dkv3[...].astype(F32)
     query_raw = head_back(query_grad, raw[:, :HEAD_DIM], gains[0:1, :], FACTOR)
     key_raw = head_back(both[:, :HEAD_DIM], raw[:, HEAD_DIM:], gains[1:2, :], 1.0)
     value_raw = both[:, HEAD_DIM:].astype(BF16)
-    grads = jnp.concatenate([query_raw, key_raw, value_raw], axis=1)
-    grads = jnp.where(y == GRAD_ROLE, jnp.zeros_like(grads), grads)
-    sent[...] = nt(grads, weight[pl.ds(there, half), :]).astype(BF16)
-    kept[...] = nt(grads, weight[pl.ds(here, half), :]).astype(BF16)
-
-
-def pair_kernel(kept, got, p0, p1, p2, p3):
+    joined = jnp.concatenate([query_raw, key_raw, value_raw], axis=1)
+    grads[...] = jnp.where(at[0] == GRAD_ROLE, jnp.zeros_like(joined), joined)
+
+
+def spread_kernel(mine, other, w_mine, w_other, p0, p1, p2, p3):
     block = p0.shape[0]
+    total = nt(mine[...], w_mine[...]) + nt(other[...], w_other[...])
     for n, out in enumerate((p0, p1, p2, p3)):
-        at = slice(n * block, (n + 1) * block)
-        out[...] = (kept[at, :].astype(F32) + got[at, :].astype(F32)).astype(BF16)
+        out[...] = total[n * block : (n + 1) * block, :].astype(BF16)
 
 
 def line_kernel(p0, p1, p2, p3, out):
@@ -274,11 +282,18 @@
     out[...] = total.astype(BF16)
 
 
-def last_kernel(at, hidden, mine, other, scale, out, grad):
-    half = mine.shape[1]
+def last_kernel(at, hidden, a0, a1, b0, b1, scale, o0, o1, o2, o3, out, outproj, grad):
+    half = a0.shape[1]
+    for j, part in enumerate((o0, o1, o2, o3)):
+        head = lax.rem(at[0] + j, ROLES)
+
+        @pl.when(head < GRAD_ROLE)
+        def _():
+            outproj[:, pl.ds(pl.multiple_of(head * HEAD_DIM, HEAD_DIM), HEAD_DIM)] = part[...]
+
     here, there = half_start(at[1], half), half_start(1 - at[1], half)
-    grad[:, pl.ds(here, half)] = mine[...].astype(F32)
-    grad[:, pl.ds(there, half)] = other[...].astype(F32)
+    grad[:, pl.ds(here, half)] = a0[...].astype(F32) + a1[...].astype(F32)
+    grad[:, pl.ds(there, half)] = b0[...].astype(F32) + b1[...].astype(F32)
     values = hidden[...].astype(F32)
     center = values - jnp.mean(values, axis=-1, keepdims=True)
     inverse = lax.rsqrt(jnp.mean(center * center, axis=-1, keepdims=True) + EPSILON)
@@ -308,31 +323,35 @@
     own_rows = query_weight.shape[0]
     columns = 3 * HEAD_DIM
     y = lax.axis_index("y")
-    at = jnp.stack([y, lax.axis_index("core")]).astype(jnp.int32)
+    at = jnp.stack([y, lax.axis_index("core"), lax.axis_index(("z", "x"))]).astype(jnp.int32)
     scale, shift, gate = mod_scale[None], mod_shift[None], branch_gate[None]
     gains = jnp.stack(
         [lax.dynamic_slice_in_dim(g, y * HEAD_DIM, HEAD_DIM) for g in (query_gain, key_gain)]
     )
 
-    (packed,) = call(pack_kernel, [((ROLES, own_rows, columns), BF16)], (), 0)(
-        query_weight, key_weight, value_weight, output_weight
+    packed = call(pack_kernel, [((own_rows, columns), BF16)] * ROLES)(
+        at, query_weight, key_weight, value_weight, output_weight
     )
-    packed = exchanged(packed, "y")
-    packed = jnp.broadcast_to(packed[None], (8, *packed.shape))
-    pieces = exchanged(packed, ("z", "x"))
-
-    own, s1, s2, s3, *cots = call(
+    packed = [packed[0]] + [shifted(p, "y", j) for j, p in zip((1, 2, 3), packed[1:])]
+    packed = jnp.stack(packed)
+    pieces = [packed]
+    for dz, dx in PLANE_ORDER:
+        moves = [(4 * z + x, 4 * ((z + dz) % 2) + (x + dx) % 4) for z in range(2) for x in range(4)]
+        pieces.append(lax.ppermute(packed, ("z", "x"), moves))
+
+    own, s1, s2, s3, branch, branch_half = call(
         norm_kernel,
-        [((rows, width), BF16)] + [((rows, half), BF16)] * 3 + [((rows, width // ROLES), BF16)] * 4,
+        [((rows, width), BF16)] + [((rows, half), BF16)] * 3 + [((rows, width), BF16), ((rows, half), BF16)],
     )(at, hidden, cotangent, scale, shift, gate)
     mine = [shifted(s, "y", j) for j, s in ((1, s1), (2, s2), (3, s3))]
     other = [shifted(m, "core", 1) for m in mine]
-    query, kv, raw, *grad_sent, weight = call(
+    query, kv, raw, *grad_sent, w_here, w_there = call(
         project_kernel,
         [((line, HEAD_DIM), BF16), ((line, 2 * HEAD_DIM), BF16), ((line, 2 * HEAD_DIM), F32)]
         + [((line, HEAD_DIM), BF16)] * 3
-        + [((width, columns), BF16)],
-    )(at, own, *mine, *other, pieces, gains)
+        + [((half, columns), BF16)] * 2,
+    )(at, own, *mine, *other, *pieces, gains)
+    w_other = shifted(w_there, "core", 1)
 
     kvs = [kv] + [shifted(kv, "x", j) for j in (1, 2, 3)]
     query_there = shifted(query, "z", 1)
@@ -366,28 +385,30 @@
     dq_got = shifted(dq1, "z", 1)
     dkv_got = [shifted(d, "x", -j) for j, d in zip((1, 2, 3), dkvs[1:])]
 
-    cots = [cots[0]] + [shifted(c, "y", j) for j, c in zip((1, 2, 3), cots[1:])]
-    mixes = call(mix_kernel, [((line, HEAD_DIM), BF16)] * 4, (), 0)(stats, sent_stats, mix_own, mix_got)
-    mixes = [mixes[0]] + [shifted(m, "y", j, range(3)) for j, m in zip((1, 2, 3), mixes[1:])]
-    (partial,) = call(
-        outproj_kernel, [((8, own_rows, columns), BF16)], [pltpu.VMEM((line, ROLES * HEAD_DIM), BF16)]
-    )(at, *mixes, *cots)
+    cots = [shifted(branch_half, "y", j) for j in (1, 2, 3)]
+    cots_other = [shifted(c, "core", 1) for c in cots]
+    (partial,) = call(outproj_kernel, [((8, ROLES, own_rows, HEAD_DIM), BF16)])(
+        at, stats, sent_stats, mix_own, mix_got, branch, *cots, *cots_other
+    )
     partial = exchanged(partial, ("z", "x"))
-    (outproj_grad,) = call(sum_kernel, [((own_rows, columns), F32)], (), 0)(partial)
-
-    kept, sent = call(back_kernel, [((line, half), BF16)] * 2)(
-        at, dq0, dq_got, dkvs[0], *dkv_got, raw, gains, weight
+    summed = call(sum_kernel, [((own_rows, HEAD_DIM), F32)] * ROLES)(at, partial)
+    summed = [summed[0]] + [shifted(p, "y", -j, range(3)) for j, p in zip((1, 2, 3), summed[1:])]
+
+    (raw_grads,) = call(back_kernel, [((line, columns), BF16)])(
+        at, dq0, dq_got, dkvs[0], *dkv_got, raw, gains
     )
-    got = shifted(sent, "core", 1)
-    parts = call(pair_kernel, [((rows, half), BF16)] * 4, (), 0)(kept, got)
+    raw_other = shifted(raw_grads, "core", 1)
+    parts = call(spread_kernel, [((rows, half), BF16)] * 4, (), 0)(raw_grads, raw_other, w_here, w_other)
     parts = [parts[0]] + [shifted(p, "y", -j, range(3)) for j, p in zip((1, 2, 3), parts[1:])]
     (chip,) = call(line_kernel, [((rows, half), BF16)], (), 0)(*parts)
     chip_got = shifted(chip, "zlo", 1)
-    total = (chip.astype(F32) + chip_got.astype(F32)).astype(BF16)
-    total_other = shifted(total, "core", 1)
-    (hidden_grad,) = call(
-        last_kernel, [((rows, width), BF16)], [pltpu.VMEM((rows, width), F32)]
-    )(at, hidden, total, total_other, scale)
+    chip_other = shifted(chip, "core", 1)
+    got_other = shifted(chip_got, "core", 1)
+    hidden_grad, outproj_grad = call(
+        last_kernel,
+        [((rows, width), BF16), ((own_rows, columns), F32)],
+        [pltpu.VMEM((rows, width), F32)],
+    )(at, hidden, chip, chip_got, chip_other, got_other, scale, *summed)
     return (hidden_grad, outproj_grad)
 
 

time: 221 us -> 221 us (level)
  starting transfers between devices: 76.6 us -> 98.2 us
  blocking collectives: 10.9 us -> 0 us
  waiting for transfers between devices: 65.8 us -> 61.2 us
  Pallas kernels: 50 us -> 47.1 us
  local copies, waits for them, and re-layouts: 11.3 us -> 9.05 us
    ppermute x32 -> x40, waiting for transfers between devices: 57.6 us -> 29.6 us  [shifted(): lax.ppermute(array, axis, [(i, (i + shift) % peers) for i in sources])]
    ppermute x0 -> x7, waiting for transfers between devices: none -> 18.8 us  [body(): pieces.append(lax.ppermute(packed, ('z', 'x'), moves))]
    ppermute x0 -> x7, starting transfers between devices: none -> 14.6 us  [body(): pieces.append(lax.ppermute(packed, ('z', 'x'), moves))]
    ppermute x32 -> x40, starting transfers between devices: 65.8 us -> 79.2 us  [shifted(): lax.ppermute(array, axis, [(i, (i + shift) % peers) for i in sources])]
    all_to_all x1 -> x0, blocking collectives: 10.9 us -> none  [exchanged(): return lax.all_to_all(array, axes, 0, 0, tiled=True)]
    all_to_all x2 -> x1, starting transfers between devices: 10.9 us -> 4.4 us  [exchanged(): return lax.all_to_all(array, axes, 0, 0, tiled=True)]
    all_to_all x2 -> x1, waiting for transfers between devices: 8.16 us -> 12.8 us  [exchanged(): return lax.all_to_all(array, axes, 0, 0, tiled=True)]
    pallas_call x12 -> x11, Pallas kernels: 50 us -> 47.1 us  [run(): pl.pallas_call(kernel, out_shape=tuple((jax.ShapeDtypeStruct(s, t) for s,...]
  transfers between devices with their start and end apart: 34 -> 48, of which waited for: 18 -> 17; matrix products, arithmetic and copies ran while one was open for 1% -> 1% of each run, Pallas kernels for 5% -> 16%
where the time goes in v1:
time: 221 us; the launch traced here: 219 us
  starting transfers between devices  98.2 us (44%)
  waiting for transfers between devices  61.2 us (28%)
  Pallas kernels  47.1 us (21%)
  local copies, waits for them, and re-layouts  9.05 us (4%)
    ppermute x40, starting transfers between devices, shifted(): lax.ppermute(array, axis, [(i, (i + shift) % peers) for i in sources])  79.2 us
    pallas_call x11, Pallas kernels, run(): pl.pallas_call(kernel, out_shape=tuple((jax.ShapeDtypeStruct(s, t) for s,...  47.1 us
    ppermute x40, waiting for transfers between devices, shifted(): lax.ppermute(array, axis, [(i, (i + shift) % peers) for i in sources])  29.6 us
    ppermute x7, waiting for transfers between devices, body(): pieces.append(lax.ppermute(packed, ('z', 'x'), moves))  18.8 us
    ppermute x7, starting transfers between devices, body(): pieces.append(lax.ppermute(packed, ('z', 'x'), moves))  14.6 us
    all_to_all x1, waiting for transfers between devices, exchanged(): return lax.all_to_all(array, axes, 0, 0, tiled=True)  12.8 us
    unnamed x90, local copies, waits for them, and re-layouts  8.28 us
  transfers between devices with their start and end apart: 48, of which 17 were waited for; matrix products, arithmetic and copies ran while one was open for 1% of the time, Pallas kernels for 16%

profile of v1, /device:TPU:1, one launch (start us, length us, event | category | flops | bytes accessed | tf_op | source)
XLA Modules:
  0.0 218.8 jit_solution(6431725222526818346)
XLA Ops:
  1.2 1.8 shard_map.123
  3.1 2.1 collective-permute-start.6
  5.2 2.6 %collective-permute-start.7 = (bf16[96,384]{1,0:T(8,128)(2,1)}, bf16[96,384]{1,0:T(8,128)(2,1)S(1)}, u32[]{:S(2)}, u32[]{:S(2)}) collective-permute-start(bf16[96,384]{1,0:T(8,128)(2,1)} %get-tuple-element.43), channel_id=1, source_target_pairs={{0,64},{32,96},{64,0},{96,32},{1,65},{33,97},{65,1},{97,33},{2,66}... | collective-permute-start | bytes 221192 | tf_op jit(solution)/shard_map/ppermute | solution.py:37
  8.9 2.1 collective-permute-done.7
  12.5 6.2 %collective-permute-start.15 = (bf16[4,96,384]{2,1,0:T(8,128)(2,1)S(1)}, bf16[4,96,384]{2,1,0:T(8,128)(2,1)S(1)}, u32[]{:S(2)}, u32[]{:S(2)}) collective-permute-start(bf16[4,96,384]{2,1,0:T(8,128)(2,1)S(1)} %pad_maximum_fusion.w0), channel_id=1, source_target_pairs={{0,24},{4,28},{8,16},{12,20},{16,8},{20,12},{24,0},{28,4},{1,25},{... | collective-permute-start | bytes 884744 | tf_op jit(solution)/shard_map/ppermute | solution.py:340
  20.5 4.5 %shard_map.122 = (bf16[128,3072]{1,0:T(8,128)(2,1)}, bf16[128,1536]{1,0:T(8,128)(2,1)}, bf16[128,1536]{1,0:T(8,128)(2,1)}, bf16[128,1536]{1,0:T(8,128)(2,1)}, bf...) custom-call(s32[3]{0:T(128)} %pad_add_fusion.at, bf16[128,3072]{1,0:T(8,128)(2,1)} %hidden.3, bf16[128,3072]{1,0:T(8,128)(2,1)} %cot.1, ...), custom_call_target="tpu_custom_call" | custom-call | tf_op jit(solution)/shard_map/pallas_call | solution.py:48
  25.0 3.3 %collective-permute-start.1 = (bf16[128,1536]{1,0:T(8,128)(2,1)}, bf16[128,1536]{1,0:T(8,128)(2,1)S(1)}, u32[]{:S(2)}, u32[]{:S(2)}) collective-permute-start(bf16[128,1536]{1,0:T(8,128)(2,1)} %get-tuple-element.39), channel_id=1, source_target_pairs={{0,64},{32,96},{64,0},{96,32},{1,65},{33,97},{65,1},{97,33},{2,66}... | collective-permute-start | bytes 1179656 | tf_op jit(solution)/shard_map/ppermute | solution.py:37
  28.4 1.9 collective-permute-done.14.w6
  30.7 9.0 %collective-permute-done.13.w5 = bf16[4,96,384]{2,1,0:T(8,128)(2,1)S(1)} collective-permute-done((bf16[4,96,384]{2,1,0:T(8,128)(2,1)S(1)}, bf16[4,96,384]{2,1,0:T(8,128)(2,1)S(1)}, u32[]{:S(2)}, u32[]{:S(2)}) %collective-permute-start.13) | collective-permute-done | bytes 294944 | tf_op jit(solution)/shard_map/ppermute | solution.py:340
  39.7 2.6 %collective-permute-start.11 = (bf16[4,96,384]{2,1,0:T(8,128)(2,1)S(1)}, bf16[4,96,384]{2,1,0:T(8,128)(2,1)S(1)}, u32[]{:S(2)}, u32[]{:S(2)}) collective-permute-start(bf16[4,96,384]{2,1,0:T(8,128)(2,1)S(1)} %pad_maximum_fusion.w0), channel_id=1, source_target_pairs={{0,12},{4,0},{8,4},{12,8},{16,28},{20,16},{24,20},{28,24},{1,13},{... | collective-permute-start | bytes 884744 | tf_op jit(solution)/shard_map/ppermute | solution.py:340
  43.5 3.5 %collective-permute-start.4 = (bf16[128,1536]{1,0:T(8,128)(2,1)S(1)}, bf16[128,1536]{1,0:T(8,128)(2,1)S(1)}, u32[]{:S(2)}, u32[]{:S(2)}) collective-permute-start(bf16[128,1536]{1,0:T(8,128)(2,1)S(1)} %collective-permute-done.1.m2), channel_id=1, source_target_pairs={{0,1},{1,0},{2,3},{3,2},{4,5},{5,4},{6,7},{7,6},{8,9},{9,8},{10,11... | collective-permute-start | bytes 1179656 | tf_op jit(solution)/shard_map/ppermute | solution.py:37
  47.0 3.6 %collective-permute-start.10 = (bf16[4,96,384]{2,1,0:T(8,128)(2,1)S(1)}, bf16[4,96,384]{2,1,0:T(8,128)(2,1)}, u32[]{:S(2)}, u32[]{:S(2)}) collective-permute-start(bf16[4,96,384]{2,1,0:T(8,128)(2,1)S(1)} %pad_maximum_fusion.w0), channel_id=1, source_target_pairs={{0,16},{4,20},{8,24},{12,28},{16,0},{20,4},{24,8},{28,12},{1,17},{... | collective-permute-start | bytes 884744 | tf_op jit(solution)/shard_map/ppermute | solution.py:340
  52.7 5.0 %collective-permute-done.10.w2 = bf16[4,96,384]{2,1,0:T(8,128)(2,1)} collective-permute-done((bf16[4,96,384]{2,1,0:T(8,128)(2,1)S(1)}, bf16[4,96,384]{2,1,0:T(8,128)(2,1)}, u32[]{:S(2)}, u32[]{:S(2)}) %collective-permute-start.10) | collective-permute-done | bytes 294944 | tf_op jit(solution)/shard_map/ppermute | solution.py:340
  57.7 2.8 %collective-permute-done.9.w1 = bf16[4,96,384]{2,1,0:T(8,128)(2,1)} collective-permute-done((bf16[4,96,384]{2,1,0:T(8,128)(2,1)S(1)}, bf16[4,96,384]{2,1,0:T(8,128)(2,1)}, u32[]{:S(2)}, u32[]{:S(2)}) %collective-permute-start.9) | collective-permute-done | bytes 294944 | tf_op jit(solution)/shard_map/ppermute | solution.py:340
  61.6 6.0 %shard_map.124 = (bf16[512,128]{1,0:T(8,128)(2,1)}, bf16[512,256]{1,0:T(8,128)(2,1)}, f32[512,256]{1,0:T(8,128)}, bf16[512,128]{1,0:T(8,128)(2,1)}, bf16[512,128...) custom-call(s32[3]{0:T(128)} %pad_add_fusion.at, ...), custom_call_target="tpu_custom_call" | custom-call | tf_op jit(solution)/shard_map/pallas_call | solution.py:48
  71.9 2.8 %collective-permute-done.17 = bf16[512,128]{1,0:T(8,128)(2,1)S(1)} collective-permute-done((bf16[512,128]{1,0:T(8,128)(2,1)}, bf16[512,128]{1,0:T(8,128)(2,1)S(1)}, u32[]{:S(2)}, u32[]{:S(2)}) %collective-permute-start.17) | collective-permute-done | bytes 131104 | tf_op jit(solution)/shard_map/ppermute | solution.py:37
  74.7 3.5 %collective-permute-start.16 = (bf16[512,128]{1,0:T(8,128)(2,1)}, bf16[512,128]{1,0:T(8,128)(2,1)S(1)}, u32[]{:S(2)}, u32[]{:S(2)}) collective-permute-start(bf16[512,128]{1,0:T(8,128)(2,1)} %get-tuple-element.45.q0), channel_id=1, source_target_pairs={{0,16},{16,0},{1,17},{17,1},{2,18},{18,2},{3,19},{19,3},{4,20},{20... | collective-permute-start | bytes 393224 | tf_op jit(solution)/shard_map/ppermute | solution.py:37
  78.3 2.5 %collective-permute-done.16.q1 = bf16[512,128]{1,0:T(8,128)(2,1)S(1)} collective-permute-done((bf16[512,128]{1,0:T(8,128)(2,1)}, bf16[512,128]{1,0:T(8,128)(2,1)S(1)}, u32[]{:S(2)}, u32[]{:S(2)}) %collective-permute-start.16) | collective-permute-done | bytes 131104 | tf_op jit(solution)/shard_map/ppermute | solution.py:37
  80.8 3.0 %collective-permute-start.20 = (bf16[512,128]{1,0:T(8,128)(2,1)S(1)}, bf16[512,128]{1,0:T(8,128)(2,1)S(1)}, u32[]{:S(2)}, u32[]{:S(2)}) collective-permute-start(bf16[512,128]{1,0:T(8,128)(2,1)S(1)} %add_add_fusion.g0), channel_id=1, source_target_pairs={{0,16},{16,0},{1,17},{17,1},{2,18},{18,2},{3,19},{19,3},{4,20},{20... | collective-permute-start | bytes 393224 | tf_op jit(solution)/shard_map/ppermute | solution.py:37
  83.8 3.2 %collective-permute-done.20.g1 = bf16[512,128]{1,0:T(8,128)(2,1)S(1)} collective-permute-done((bf16[512,128]{1,0:T(8,128)(2,1)S(1)}, bf16[512,128]{1,0:T(8,128)(2,1)S(1)}, u32[]{:S(2)}, u32[]{:S(2)}) %collective-permute-start.20) | collective-permute-done | bytes 131104 | tf_op jit(solution)/shard_map/ppermute | solution.py:37
  87.0 2.7 %collective-permute-done.21.kv1 = bf16[512,256]{1,0:T(8,128)(2,1)S(1)} collective-permute-done((bf16[512,256]{1,0:T(8,128)(2,1)}, bf16[512,256]{1,0:T(8,128)(2,1)S(1)}, u32[]{:S(2)}, u32[]{:S(2)}) %collective-permute-start.21) | collective-permute-done | bytes 262176 | tf_op jit(solution)/shard_map/ppermute | solution.py:37
  90.4 7.1 %shard_map.125 = (f32[8,1024]{1,0:T(8,128)}, f32[128,512]{1,0:T(8,128)}, bf16[128,512]{1,0:T(8,128)(2,1)}) custom-call(bf16[512,128]{1,0:T(8,128)(2,1)} %get-tuple-element.45.q0, bf16[512,128]{1,0:T(8,128)(2,1)} %copy-done.8, bf16[512,128]{1,0:T(8,128)(2,1)} %copy-done.4, bf16[512,128]{1,0:T(8,128)(2,1)} %copy-done.9, ...), custom_call_target="tpu_custom_call" | custom-call | tf_op jit(solution)/shard_map/pallas_call | solution.py:48
  98.9 3.1 %collective-permute-done.24.sent = f32[8,1024]{1,0:T(8,128)S(1)} collective-permute-done((f32[8,1024]{1,0:T(8,128)}, f32[8,1024]{1,0:T(8,128)S(1)}, u32[]{:S(2)}, u32[]{:S(2)}) %collective-permute-start.24) | collective-permute-done | bytes 32800 | tf_op jit(solution)/shard_map/ppermute | solution.py:37
  102.6 8.4 %shard_map.126 = (f32[512,128]{1,0:T(8,128)}, bf16[512,128]{1,0:T(8,128)(2,1)}, f32[512,256]{1,0:T(8,128)}, bf16[512,256]{1,0:T(8,128)(2,1)}, bf16[512,256]{1,0:T(8,128)(2,1)}, /*index=5*/bf16[512,256]{1,0:T(8,128)(2,1)}) custom-call(bf16[512,128]{1,0:T(8,128)(2,1)} %get-tuple-element.45.q0, bf16[512,128]{1,0:T(8,128)(2,1)} %copy-done.8, ...), custom_call_target="tpu_custom_call" | custom-call | tf_op jit(solution)/shard_map/pallas_call | solution.py:48
  112.5 2.0 collective-permute-start.25
  114.5 3.5 %collective-permute-done.25.dq1 = bf16[512,128]{1,0:T(8,128)(2,1)S(1)} collective-permute-done((bf16[512,128]{1,0:T(8,128)(2,1)}, bf16[512,128]{1,0:T(8,128)(2,1)S(1)}, u32[]{:S(2)}, u32[]{:S(2)}) %collective-permute-start.25) | collective-permute-done | bytes 131104 | tf_op jit(solution)/shard_map/ppermute | solution.py:37
  118.2 2.7 %collective-permute-done.28.dkv3 = bf16[512,256]{1,0:T(8,128)(2,1)S(1)} collective-permute-done((bf16[512,256]{1,0:T(8,128)(2,1)}, bf16[512,256]{1,0:T(8,128)(2,1)S(1)}, u32[]{:S(2)}, u32[]{:S(2)}) %collective-permute-start.28) | collective-permute-done | bytes 262176 | tf_op jit(solution)/shard_map/ppermute | solution.py:37
  121.6 2.9 %shard_map.127.mine = bf16[512,384]{1,0:T(8,128)(2,1)} custom-call(s32[3]{0:T(128)} %pad_add_fusion.at, f32[512,128]{1,0:T(8,128)} %get-tuple-element.51.dq0, bf16[512,128]{1,0:T(8,128)(2,1)} %copy-done.39, f32[512,256]{1,0:T(8,128)} %get-tuple-element.53.dkv0, bf16[512,256]{1,0:T(8,128)(2,1)} %copy-done.34, bf16[512,256]{1,0:T(8,128)(2,1)} %copy-done.35, ...), custom_call_target="tpu_custom_call" | custom-call | tf_op jit(solution)/shard_map/pallas_call | solution.py:48
  124.4 7.6 %collective-permute-start.29 = (bf16[512,384]{1,0:T(8,128)(2,1)}, bf16[512,384]{1,0:T(8,128)(2,1)S(1)}, u32[]{:S(2)}, u32[]{:S(2)}) collective-permute-start(bf16[512,384]{1,0:T(8,128)(2,1)} %shard_map.127.mine), channel_id=1, source_target_pairs={{0,1},{1,0},{2,3},{3,2},{4,5},{5,4},{6,7},{7,6},{8,9},{9,8},{10,11... | collective-permute-start | bytes 1179656 | tf_op jit(solution)/shard_map/ppermute | solution.py:37
  132.1 2.2 %collective-permute-start.40 = (bf16[128,1536]{1,0:T(8,128)(2,1)S(1)}, bf16[128,1536]{1,0:T(8,128)(2,1)S(1)}, u32[]{:S(2)}, u32[]{:S(2)}) collective-permute-start(bf16[128,1536]{1,0:T(8,128)(2,1)S(1)} %copy-done.43), channel_id=1, source_target_pairs={{0,96},{32,0},{64,32},{96,64},{1,97},{33,1},{65,33},{97,65},{2,98}... | collective-permute-start | bytes 1179656 | tf_op jit(solution)/shard_map/ppermute | solution.py:37
  137.0 4.8 %shard_map.128 = (bf16[128,1536]{1,0:T(8,128)(2,1)}, bf16[128,1536]{1,0:T(8,128)(2,1)}, bf16[128,1536]{1,0:T(8,128)(2,1)}, bf16[128,1536]{1,0:T(8,128)(2,1)}) custom-call(bf16[512,384]{1,0:T(8,128)(2,1)} %shard_map.127.mine, bf16[512,384]{1,0:T(8,128)(2,1)} %copy-done.22, bf16[1536,384]{1,0:T(8,128)(2,1)} %get-tuple-element.58.w_mine, ...), custom_call_target="tpu_custom_call" | custom-call | tf_op jit(solution)/shard_map/pallas_call | solution.py:48
  141.7 4.6 %collective-permute-start.31 = (bf16[128,1536]{1,0:T(8,128)(2,1)}, bf16[128,1536]{1,0:T(8,128)(2,1)S(1)}, u32[]{:S(2)}, u32[]{:S(2)}) collective-permute-start(bf16[128,1536]{1,0:T(8,128)(2,1)} %get-tuple-element.61), channel_id=1, source_target_pairs={{0,96},{32,0},{64,32},{1,97},{33,1},{65,33},{2,98},{34,2},{66,34},... | collective-permute-start | bytes 1179656 | tf_op jit(solution)/shard_map/ppermute | solution.py:37
  146.3 2.2 collective-permute-start.32
  148.5 1.6 collective-permute-start.33
  150.2 6.6 %collective-permute-start.43 = (bf16[128,1536]{1,0:T(8,128)(2,1)S(1)}, bf16[128,1536]{1,0:T(8,128)(2,1)S(1)}, u32[]{:S(2)}, u32[]{:S(2)}) collective-permute-start(bf16[128,1536]{1,0:T(8,128)(2,1)S(1)} %collective-permute-done.40.c3), channel_id=1, source_target_pairs={{0,1},{1,0},{2,3},{3,2},{4,5},{5,4},{6,7},{7,6},{8,9},{9,8},{10,11... | collective-permute-start | bytes 1179656 | tf_op jit(solution)/shard_map/ppermute | solution.py:37
  156.9 3.4 %collective-permute-done.31.p1 = bf16[128,1536]{1,0:T(8,128)(2,1)S(1)} collective-permute-done((bf16[128,1536]{1,0:T(8,128)(2,1)}, bf16[128,1536]{1,0:T(8,128)(2,1)S(1)}, u32[]{:S(2)}, u32[]{:S(2)}) %collective-permute-start.31) | collective-permute-done | bytes 393248 | tf_op jit(solution)/shard_map/ppermute | solution.py:37
  160.4 8.7 %collective-permute-start.41 = (bf16[128,1536]{1,0:T(8,128)(2,1)S(1)}, bf16[128,1536]{1,0:T(8,128)(2,1)S(1)}, u32[]{:S(2)}, u32[]{:S(2)}) collective-permute-start(bf16[128,1536]{1,0:T(8,128)(2,1)S(1)} %collective-permute-done.38.c1), channel_id=1, source_target_pairs={{0,1},{1,0},{2,3},{3,2},{4,5},{5,4},{6,7},{7,6},{8,9},{9,8},{10,11... | collective-permute-start | bytes 1179656 | tf_op jit(solution)/shard_map/ppermute | solution.py:37
  169.1 2.8 %collective-permute-start.37 = (bf16[128,512]{1,0:T(8,128)(2,1)S(1)}, bf16[128,512]{1,0:T(8,128)(2,1)S(1)}, u32[]{:S(2)}, u32[]{:S(2)}) collective-permute-start(bf16[128,512]{1,0:T(8,128)(2,1)S(1)} %copy-done.44), channel_id=1, source_target_pairs={{0,16},{16,0},{1,17},{17,1},{2,18},{18,2},{3,19},{19,3},{4,20},{20... | collective-permute-start | bytes 393224 | tf_op jit(solution)/shard_map/ppermute | solution.py:37
  172.6 2.3 %shard_map.129.a0 = bf16[128,1536]{1,0:T(8,128)(2,1)} custom-call(bf16[128,1536]{1,0:T(8,128)(2,1)} %get-tuple-element.60.p0, bf16[128,1536]{1,0:T(8,128)(2,1)} %copy-done.25, bf16[128,1536]{1,0:T(8,128)(2,1)} %copy-done.27, bf16[128,1536]{1,0:T(8,128)(2,1)} %copy-done.28), custom_call_target="tpu_custom_call" | custom-call | tf_op jit(solution)/shard_map/pallas_call | solution.py:48
  176.9 3.6 %shard_map.130 = bf16[8,4,96,128]{3,2,1,0:T(8,128)(2,1)} custom-call(s32[3]{0:T(128)} %pad_add_fusion.at, f32[8,1024]{1,0:T(8,128)} %get-tuple-element.50.stats, f32[8,1024]{1,0:T(8,128)} %copy-done.37, f32[128,512]{1,0:T(8,128)} %get-tuple-element.64.own, bf16[128,512]{1,0:T(8,128)(2,1)} %copy-done.38, bf16[128,3072]{1,0:T(8,128)(2,1)} %get-tuple-element.66.branch, ...), custom_call_target="tpu_custom_call" | custom-call | tf_op jit(solution)/shard_map/pallas_call | solution.py:48
  180.5 4.4 %all-to-all-start = ((bf16[8,4,96,128]{3,2,1,0:T(8,128)(2,1)}), bf16[8,4,96,128]{3,2,1,0:T(8,128)(2,1)S(1)}, u32[]{:S(2)}, u32[]{:S(2)}) async-start(bf16[8,4,96,128]{3,2,1,0:T(8,128)(2,1)} %shard_map.130), calls=%async_computation | async-start | bytes 1572864 | tf_op jit(solution)/shard_map/all_to_all | solution.py:41
  186.6 12.8 %all-to-all-done.parts = bf16[8,4,96,128]{3,2,1,0:T(8,128)(2,1)S(1)} async-done(((bf16[8,4,96,128]{3,2,1,0:T(8,128)(2,1)}), bf16[8,4,96,128]{3,2,1,0:T(8,128)(2,1)S(1)}, u32[]{:S(2)}, u32[]{:S(2)}) %all-to-all-start) | async-done | bytes 786464 | tf_op jit(solution)/shard_map/all_to_all | solution.py:41
  200.3 1.9 shard_map.131
  202.2 5.2 %collective-permute-start.44 = (f32[96,128]{1,0:T(8,128)}, f32[96,128]{1,0:T(8,128)S(1)}, u32[]{:S(2)}, u32[]{:S(2)}) collective-permute-start(f32[96,128]{1,0:T(8,128)} %get-tuple-element.69), channel_id=1, source_target_pairs={{0,96},{32,0},{64,32},{1,97},{33,1},{65,33},{2,98},{34,2},{66,34},... | collective-permute-start | bytes 147464 | tf_op jit(solution)/shard_map/ppermute | solution.py:37
  207.3 1.9 collective-permute-start.45
  209.3 1.9 collective-permute-start.46
  211.1 2.7 %collective-permute-done.45.o2 = f32[96,128]{1,0:T(8,128)S(1)} collective-permute-done((f32[96,128]{1,0:T(8,128)}, f32[96,128]{1,0:T(8,128)S(1)}, u32[]{:S(2)}, u32[]{:S(2)}) %collective-permute-start.45) | collective-permute-done | bytes 49184 | tf_op jit(solution)/shard_map/ppermute | solution.py:37
  214.8 4.0 %shard_map.132 = (bf16[128,3072]{1,0:T(8,128)(2,1)}, f32[96,384]{1,0:T(8,128)}) custom-call(s32[3]{0:T(128)} %pad_add_fusion.at, bf16[128,3072]{1,0:T(8,128)(2,1)} %hidden.3, bf16[128,1536]{1,0:T(8,128)(2,1)} %shard_map.129.a0, bf16[128,1536]{1,0:T(8,128)(2,1)} %copy-done.23, bf16[128,1536]{1,0:T(8,128)(2,1)} %copy-done.24, bf16[128,1536]{1,0:T(8,128)(2,1)} %copy-done.26, ...), custom_call_target="tpu_custom_call" | custom-call | tf_op jit(solution)/shard_map/pallas_call | solution.py:48
  (154 shorter events, 28.0 us)
Async XLA Ops:
  3.1 5.8 %collective-permute-start.6 = (bf16[96,384]{1,0:T(8,128)(2,1)}, bf16[96,384]{1,0:T(8,128)(2,1)S(1)}, u32[]{:S(2)}, u32[]{:S(2)}) collective-permute-start(bf16[96,384]{1,0:T(8,128)(2,1)} %get-tuple-element.42), channel_id=1, source_target_pairs={{0,32},{32,64},{64,96},{96,0},{1,33},{33,65},{65,97},{97,1},{2,34}... | collective-permute-start | bytes 221192 | tf_op jit(solution)/shard_map/ppermute | solution.py:37
  5.2 5.8 %collective-permute-start.7 = (bf16[96,384]{1,0:T(8,128)(2,1)}, bf16[96,384]{1,0:T(8,128)(2,1)S(1)}, u32[]{:S(2)}, u32[]{:S(2)}) collective-permute-start(bf16[96,384]{1,0:T(8,128)(2,1)} %get-tuple-element.43), channel_id=1, source_target_pairs={{0,64},{32,96},{64,0},{96,32},{1,65},{33,97},{65,1},{97,33},{2,66}... | collective-permute-start | bytes 221192 | tf_op jit(solution)/shard_map/ppermute | solution.py:37
  7.8 3.7 %collective-permute-start.8 = (bf16[96,384]{1,0:T(8,128)(2,1)}, bf16[96,384]{1,0:T(8,128)(2,1)S(1)}, u32[]{:S(2)}, u32[]{:S(2)}) collective-permute-start(bf16[96,384]{1,0:T(8,128)(2,1)} %get-tuple-element.44), channel_id=1, source_target_pairs={{0,96},{32,0},{64,32},{96,64},{1,97},{33,1},{65,33},{97,65},{2,98}... | collective-permute-start | bytes 221192 | tf_op jit(solution)/shard_map/ppermute | solution.py:37
  12.5 15.8 %collective-permute-start.15 = (bf16[4,96,384]{2,1,0:T(8,128)(2,1)S(1)}, bf16[4,96,384]{2,1,0:T(8,128)(2,1)S(1)}, u32[]{:S(2)}, u32[]{:S(2)}) collective-permute-start(bf16[4,96,384]{2,1,0:T(8,128)(2,1)S(1)} %pad_maximum_fusion.w0), channel_id=1, source_target_pairs={{0,24},{4,28},{8,16},{12,20},{16,8},{20,12},{24,0},{28,4},{1,25},{... | collective-permute-start | bytes 884744 | tf_op jit(solution)/shard_map/ppermute | solution.py:340
  18.7 11.6 %collective-permute-start.14 = (bf16[4,96,384]{2,1,0:T(8,128)(2,1)S(1)}, bf16[4,96,384]{2,1,0:T(8,128)(2,1)S(1)}, u32[]{:S(2)}, u32[]{:S(2)}) collective-permute-start(bf16[4,96,384]{2,1,0:T(8,128)(2,1)S(1)} %pad_maximum_fusion.w0), channel_id=1, source_target_pairs={{0,8},{4,12},{8,0},{12,4},{16,24},{20,28},{24,16},{28,20},{1,9},{5... | collective-permute-start | bytes 884744 | tf_op jit(solution)/shard_map/ppermute | solution.py:340
  18.9 20.8 %collective-permute-start.13 = (bf16[4,96,384]{2,1,0:T(8,128)(2,1)S(1)}, bf16[4,96,384]{2,1,0:T(8,128)(2,1)S(1)}, u32[]{:S(2)}, u32[]{:S(2)}) collective-permute-start(bf16[4,96,384]{2,1,0:T(8,128)(2,1)S(1)} %pad_maximum_fusion.w0), channel_id=1, source_target_pairs={{0,28},{4,16},{8,20},{12,24},{16,12},{20,0},{24,4},{28,8},{1,29},{... | collective-permute-start | bytes 884744 | tf_op jit(solution)/shard_map/ppermute | solution.py:340
  25.0 17.4 %collective-permute-start = (bf16[128,1536]{1,0:T(8,128)(2,1)}, bf16[128,1536]{1,0:T(8,128)(2,1)S(1)}, u32[]{:S(2)}, u32[]{:S(2)}) collective-permute-start(bf16[128,1536]{1,0:T(8,128)(2,1)} %get-tuple-element.38), channel_id=1, source_target_pairs={{0,32},{32,64},{64,96},{96,0},{1,33},{33,65},{65,97},{97,1},{2,34}... | collective-permute-start | bytes 1179656 | tf_op jit(solution)/shard_map/ppermute | solution.py:37
  25.0 18.5 %collective-permute-start.1 = (bf16[128,1536]{1,0:T(8,128)(2,1)}, bf16[128,1536]{1,0:T(8,128)(2,1)S(1)}, u32[]{:S(2)}, u32[]{:S(2)}) collective-permute-start(bf16[128,1536]{1,0:T(8,128)(2,1)} %get-tuple-element.39), channel_id=1, source_target_pairs={{0,64},{32,96},{64,0},{96,32},{1,65},{33,97},{65,1},{97,33},{2,66}... | collective-permute-start | bytes 1179656 | tf_op jit(solution)/shard_map/ppermute | solution.py:37
  28.2 18.7 %collective-permute-start.2 = (bf16[128,1536]{1,0:T(8,128)(2,1)}, bf16[128,1536]{1,0:T(8,128)(2,1)S(1)}, u32[]{:S(2)}, u32[]{:S(2)}) collective-permute-start(bf16[128,1536]{1,0:T(8,128)(2,1)} %get-tuple-element.40), channel_id=1, source_target_pairs={{0,96},{32,0},{64,32},{96,64},{1,97},{33,1},{65,33},{97,65},{2,98}... | collective-permute-start | bytes 1179656 | tf_op jit(solution)/shard_map/ppermute | solution.py:37
  30.3 16.7 %collective-permute-start.12 = (bf16[4,96,384]{2,1,0:T(8,128)(2,1)S(1)}, bf16[4,96,384]{2,1,0:T(8,128)(2,1)S(1)}, u32[]{:S(2)}, u32[]{:S(2)}) collective-permute-start(bf16[4,96,384]{2,1,0:T(8,128)(2,1)S(1)} %pad_maximum_fusion.w0), channel_id=1, source_target_pairs={{0,20},{4,24},{8,28},{12,16},{16,4},{20,8},{24,12},{28,0},{1,21},{... | collective-permute-start | bytes 884744 | tf_op jit(solution)/shard_map/ppermute | solution.py:340
  39.7 10.9 %collective-permute-start.11 = (bf16[4,96,384]{2,1,0:T(8,128)(2,1)S(1)}, bf16[4,96,384]{2,1,0:T(8,128)(2,1)S(1)}, u32[]{:S(2)}, u32[]{:S(2)}) collective-permute-start(bf16[4,96,384]{2,1,0:T(8,128)(2,1)S(1)} %pad_maximum_fusion.w0), channel_id=1, source_target_pairs={{0,12},{4,0},{8,4},{12,8},{16,28},{20,16},{24,20},{28,24},{1,13},{... | collective-permute-start | bytes 884744 | tf_op jit(solution)/shard_map/ppermute | solution.py:340
  42.3 18.3 %collective-permute-start.3 = (bf16[128,1536]{1,0:T(8,128)(2,1)S(1)}, bf16[128,1536]{1,0:T(8,128)(2,1)S(1)}, u32[]{:S(2)}, u32[]{:S(2)}) collective-permute-start(bf16[128,1536]{1,0:T(8,128)(2,1)S(1)} %collective-permute-done.m1), channel_id=1, source_target_pairs={{0,1},{1,0},{2,3},{3,2},{4,5},{5,4},{6,7},{7,6},{8,9},{9,8},{10,11... | collective-permute-start | bytes 1179656 | tf_op jit(solution)/shard_map/ppermute | solution.py:37
  43.5 17.1 %collective-permute-start.4 = (bf16[128,1536]{1,0:T(8,128)(2,1)S(1)}, bf16[128,1536]{1,0:T(8,128)(2,1)S(1)}, u32[]{:S(2)}, u32[]{:S(2)}) collective-permute-start(bf16[128,1536]{1,0:T(8,128)(2,1)S(1)} %collective-permute-done.1.m2), channel_id=1, source_target_pairs={{0,1},{1,0},{2,3},{3,2},{4,5},{5,4},{6,7},{7,6},{8,9},{9,8},{10,11... | collective-permute-start | bytes 1179656 | tf_op jit(solution)/shard_map/ppermute | solution.py:37
  46.9 13.6 %collective-permute-start.5 = (bf16[128,1536]{1,0:T(8,128)(2,1)S(1)}, bf16[128,1536]{1,0:T(8,128)(2,1)S(1)}, u32[]{:S(2)}, u32[]{:S(2)}) collective-permute-start(bf16[128,1536]{1,0:T(8,128)(2,1)S(1)} %collective-permute-done.2.m3), channel_id=1, source_target_pairs={{0,1},{1,0},{2,3},{3,2},{4,5},{5,4},{6,7},{7,6},{8,9},{9,8},{10,11... | collective-permute-start | bytes 1179656 | tf_op jit(solution)/shard_map/ppermute | solution.py:37
  47.0 10.7 %collective-permute-start.10 = (bf16[4,96,384]{2,1,0:T(8,128)(2,1)S(1)}, bf16[4,96,384]{2,1,0:T(8,128)(2,1)}, u32[]{:S(2)}, u32[]{:S(2)}) collective-permute-start(bf16[4,96,384]{2,1,0:T(8,128)(2,1)S(1)} %pad_maximum_fusion.w0), channel_id=1, source_target_pairs={{0,16},{4,20},{8,24},{12,28},{16,0},{20,4},{24,8},{28,12},{1,17},{... | collective-permute-start | bytes 884744 | tf_op jit(solution)/shard_map/ppermute | solution.py:340
  51.4 9.2 %collective-permute-start.9 = (bf16[4,96,384]{2,1,0:T(8,128)(2,1)S(1)}, bf16[4,96,384]{2,1,0:T(8,128)(2,1)}, u32[]{:S(2)}, u32[]{:S(2)}) collective-permute-start(bf16[4,96,384]{2,1,0:T(8,128)(2,1)S(1)} %pad_maximum_fusion.w0), channel_id=1, source_target_pairs={{0,4},{4,8},{8,12},{12,0},{16,20},{20,24},{24,28},{28,16},{1,5},{5... | collective-permute-start | bytes 884744 | tf_op jit(solution)/shard_map/ppermute | solution.py:340
  67.6 7.1 %collective-permute-start.17 = (bf16[512,128]{1,0:T(8,128)(2,1)}, bf16[512,128]{1,0:T(8,128)(2,1)S(1)}, u32[]{:S(2)}, u32[]{:S(2)}) collective-permute-start(bf16[512,128]{1,0:T(8,128)(2,1)} %get-tuple-element.46), channel_id=1, source_target_pairs={{96,0},{97,1},{98,2},{99,3},{100,4},{101,5},{102,6},{103,7},{104,8... | collective-permute-start | bytes 393224 | tf_op jit(solution)/shard_map/ppermute | solution.py:37
  68.9 5.8 %collective-permute-start.18 = (bf16[512,128]{1,0:T(8,128)(2,1)}, bf16[512,128]{1,0:T(8,128)(2,1)S(1)}, u32[]{:S(2)}, u32[]{:S(2)}) collective-permute-start(bf16[512,128]{1,0:T(8,128)(2,1)} %get-tuple-element.47), channel_id=1, source_target_pairs={{96,32},{97,33},{98,34},{99,35},{100,36},{101,37},{102,38},{103,39... | collective-permute-start | bytes 393224 | tf_op jit(solution)/shard_map/ppermute | solution.py:37
  69.6 5.2 %collective-permute-start.19 = (bf16[512,128]{1,0:T(8,128)(2,1)}, bf16[512,128]{1,0:T(8,128)(2,1)S(1)}, u32[]{:S(2)}, u32[]{:S(2)}) collective-permute-start(bf16[512,128]{1,0:T(8,128)(2,1)} %get-tuple-element.48), channel_id=1, source_target_pairs={{96,64},{97,65},{98,66},{99,67},{100,68},{101,69},{102,70},{103,71... | collective-permute-start | bytes 393224 | tf_op jit(solution)/shard_map/ppermute | solution.py:37
  70.2 65.6 %collective-permute-start.30 = (bf16[1536,384]{1,0:T(8,128)(2,1)}, bf16[1536,384]{1,0:T(8,128)(2,1)S(1)}, u32[]{:S(2)}, u32[]{:S(2)}) collective-permute-start(bf16[1536,384]{1,0:T(8,128)(2,1)} %get-tuple-element.59), channel_id=1, source_target_pairs={{0,1},{1,0},{2,3},{3,2},{4,5},{5,4},{6,7},{7,6},{8,9},{9,8},{10,11... | collective-permute-start | bytes 3538952 | tf_op jit(solution)/shard_map/ppermute | solution.py:37
  71.9 15.2 %collective-permute-start.23 = (bf16[512,256]{1,0:T(8,128)(2,1)}, bf16[512,256]{1,0:T(8,128)(2,1)S(1)}, u32[]{:S(2)}, u32[]{:S(2)}) collective-permute-start(bf16[512,256]{1,0:T(8,128)(2,1)} %get-tuple-element.49.kv0), channel_id=1, source_target_pairs={{0,12},{4,0},{8,4},{12,8},{1,13},{5,1},{9,5},{13,9},{2,14},{6,2},{... | collective-permute-start | bytes 786440 | tf_op jit(solution)/shard_map/ppermute | solution.py:37
  74.7 12.3 %collective-permute-start.22 = (bf16[512,256]{1,0:T(8,128)(2,1)}, bf16[512,256]{1,0:T(8,128)(2,1)S(1)}, u32[]{:S(2)}, u32[]{:S(2)}) collective-permute-start(bf16[512,256]{1,0:T(8,128)(2,1)} %get-tuple-element.49.kv0), channel_id=1, source_target_pairs={{0,8},{4,12},{8,0},{12,4},{1,9},{5,13},{9,1},{13,5},{2,10},{6,14},... | collective-permute-start | bytes 786440 | tf_op jit(solution)/shard_map/ppermute | solution.py:37
  74.7 15.0 %collective-permute-start.21 = (bf16[512,256]{1,0:T(8,128)(2,1)}, bf16[512,256]{1,0:T(8,128)(2,1)S(1)}, u32[]{:S(2)}, u32[]{:S(2)}) collective-permute-start(bf16[512,256]{1,0:T(8,128)(2,1)} %get-tuple-element.49.kv0), channel_id=1, source_target_pairs={{0,4},{4,8},{8,12},{12,0},{1,5},{5,9},{9,13},{13,1},{2,6},{6,10},{... | collective-permute-start | bytes 786440 | tf_op jit(solution)/shard_map/ppermute | solution.py:37
  74.7 6.1 %collective-permute-start.16 = (bf16[512,128]{1,0:T(8,128)(2,1)}, bf16[512,128]{1,0:T(8,128)(2,1)S(1)}, u32[]{:S(2)}, u32[]{:S(2)}) collective-permute-start(bf16[512,128]{1,0:T(8,128)(2,1)} %get-tuple-element.45.q0), channel_id=1, source_target_pairs={{0,16},{16,0},{1,17},{17,1},{2,18},{18,2},{3,19},{19,3},{4,20},{20... | collective-permute-start | bytes 393224 | tf_op jit(solution)/shard_map/ppermute | solution.py:37
  80.8 6.2 %collective-permute-start.20 = (bf16[512,128]{1,0:T(8,128)(2,1)S(1)}, bf16[512,128]{1,0:T(8,128)(2,1)S(1)}, u32[]{:S(2)}, u32[]{:S(2)}) collective-permute-start(bf16[512,128]{1,0:T(8,128)(2,1)S(1)} %add_add_fusion.g0), channel_id=1, source_target_pairs={{0,16},{16,0},{1,17},{17,1},{2,18},{18,2},{3,19},{19,3},{4,20},{20... | collective-permute-start | bytes 393224 | tf_op jit(solution)/shard_map/ppermute | solution.py:37
  97.5 4.5 %collective-permute-start.24 = (f32[8,1024]{1,0:T(8,128)}, f32[8,1024]{1,0:T(8,128)S(1)}, u32[]{:S(2)}, u32[]{:S(2)}) collective-permute-start(f32[8,1024]{1,0:T(8,128)} %get-tuple-element.50.stats), channel_id=1, source_target_pairs={{0,16},{16,0},{1,17},{17,1},{2,18},{18,2},{3,19},{19,3},{4,20},{20... | collective-permute-start | bytes 98312 | tf_op jit(solution)/shard_map/ppermute | solution.py:37
  111.0 7.0 %collective-permute-start.26 = (bf16[512,256]{1,0:T(8,128)(2,1)}, bf16[512,256]{1,0:T(8,128)(2,1)S(1)}, u32[]{:S(2)}, u32[]{:S(2)}) collective-permute-start(bf16[512,256]{1,0:T(8,128)(2,1)} %get-tuple-element.54), channel_id=1, source_target_pairs={{0,12},{4,0},{8,4},{12,8},{1,13},{5,1},{9,5},{13,9},{2,14},{6,2},{... | collective-permute-start | bytes 786440 | tf_op jit(solution)/shard_map/ppermute | solution.py:37
  111.0 7.1 %collective-permute-start.27 = (bf16[512,256]{1,0:T(8,128)(2,1)}, bf16[512,256]{1,0:T(8,128)(2,1)S(1)}, u32[]{:S(2)}, u32[]{:S(2)}) collective-permute-start(bf16[512,256]{1,0:T(8,128)(2,1)} %get-tuple-element.55), channel_id=1, source_target_pairs={{0,8},{4,12},{8,0},{12,4},{1,9},{5,13},{9,1},{13,5},{2,10},{6,14},... | collective-permute-start | bytes 786440 | tf_op jit(solution)/shard_map/ppermute | solution.py:37
  112.2 8.7 %collective-permute-start.28 = (bf16[512,256]{1,0:T(8,128)(2,1)}, bf16[512,256]{1,0:T(8,128)(2,1)S(1)}, u32[]{:S(2)}, u32[]{:S(2)}) collective-permute-start(bf16[512,256]{1,0:T(8,128)(2,1)} %get-tuple-element.56), channel_id=1, source_target_pairs={{0,4},{4,8},{8,12},{12,0},{1,5},{5,9},{9,13},{13,1},{2,6},{6,10},{... | collective-permute-start | bytes 786440 | tf_op jit(solution)/shard_map/ppermute | solution.py:37
  112.5 5.5 %collective-permute-start.25 = (bf16[512,128]{1,0:T(8,128)(2,1)}, bf16[512,128]{1,0:T(8,128)(2,1)S(1)}, u32[]{:S(2)}, u32[]{:S(2)}) collective-permute-start(bf16[512,128]{1,0:T(8,128)(2,1)} %get-tuple-element.52), channel_id=1, source_target_pairs={{0,16},{16,0},{1,17},{17,1},{2,18},{18,2},{3,19},{19,3},{4,20},{20... | collective-permute-start | bytes 393224 | tf_op jit(solution)/shard_map/ppermute | solution.py:37
  124.4 11.4 %collective-permute-start.29 = (bf16[512,384]{1,0:T(8,128)(2,1)}, bf16[512,384]{1,0:T(8,128)(2,1)S(1)}, u32[]{:S(2)}, u32[]{:S(2)}) collective-permute-start(bf16[512,384]{1,0:T(8,128)(2,1)} %shard_map.127.mine), channel_id=1, source_target_pairs={{0,1},{1,0},{2,3},{3,2},{4,5},{5,4},{6,7},{7,6},{8,9},{9,8},{10,11... | collective-permute-start | bytes 1179656 | tf_op jit(solution)/shard_map/ppermute | solution.py:37
  132.1 16.4 %collective-permute-start.40 = (bf16[128,1536]{1,0:T(8,128)(2,1)S(1)}, bf16[128,1536]{1,0:T(8,128)(2,1)S(1)}, u32[]{:S(2)}, u32[]{:S(2)}) collective-permute-start(bf16[128,1536]{1,0:T(8,128)(2,1)S(1)} %copy-done.43), channel_id=1, source_target_pairs={{0,96},{32,0},{64,32},{96,64},{1,97},{33,1},{65,33},{97,65},{2,98}... | collective-permute-start | bytes 1179656 | tf_op jit(solution)/shard_map/ppermute | solution.py:37
  134.3 15.9 %collective-permute-start.39 = (bf16[128,1536]{1,0:T(8,128)(2,1)S(1)}, bf16[128,1536]{1,0:T(8,128)(2,1)S(1)}, u32[]{:S(2)}, u32[]{:S(2)}) collective-permute-start(bf16[128,1536]{1,0:T(8,128)(2,1)S(1)} %copy-done.43), channel_id=1, source_target_pairs={{0,64},{32,96},{64,0},{96,32},{1,65},{33,97},{65,1},{97,33},{2,66}... | collective-permute-start | bytes 1179656 | tf_op jit(solution)/shard_map/ppermute | solution.py:37
  135.8 21.0 %collective-permute-start.38 = (bf16[128,1536]{1,0:T(8,128)(2,1)S(1)}, bf16[128,1536]{1,0:T(8,128)(2,1)S(1)}, u32[]{:S(2)}, u32[]{:S(2)}) collective-permute-start(bf16[128,1536]{1,0:T(8,128)(2,1)S(1)} %copy-done.43), channel_id=1, source_target_pairs={{0,32},{32,64},{64,96},{96,0},{1,33},{33,65},{65,97},{97,1},{2,34}... | collective-permute-start | bytes 1179656 | tf_op jit(solution)/shard_map/ppermute | solution.py:37
  141.7 18.6 %collective-permute-start.31 = (bf16[128,1536]{1,0:T(8,128)(2,1)}, bf16[128,1536]{1,0:T(8,128)(2,1)S(1)}, u32[]{:S(2)}, u32[]{:S(2)}) collective-permute-start(bf16[128,1536]{1,0:T(8,128)(2,1)} %get-tuple-element.61), channel_id=1, source_target_pairs={{0,96},{32,0},{64,32},{1,97},{33,1},{65,33},{2,98},{34,2},{66,34},... | collective-permute-start | bytes 1179656 | tf_op jit(solution)/shard_map/ppermute | solution.py:37
  146.3 22.7 %collective-permute-start.32 = (bf16[128,1536]{1,0:T(8,128)(2,1)}, bf16[128,1536]{1,0:T(8,128)(2,1)S(1)}, u32[]{:S(2)}, u32[]{:S(2)}) collective-permute-start(bf16[128,1536]{1,0:T(8,128)(2,1)} %get-tuple-element.62), channel_id=1, source_target_pairs={{0,64},{32,96},{64,0},{1,65},{33,97},{65,1},{2,66},{34,98},{66,2},... | collective-permute-start | bytes 1179656 | tf_op jit(solution)/shard_map/ppermute | solution.py:37
  148.5 23.3 %collective-permute-start.33 = (bf16[128,1536]{1,0:T(8,128)(2,1)}, bf16[128,1536]{1,0:T(8,128)(2,1)S(1)}, u32[]{:S(2)}, u32[]{:S(2)}) collective-permute-start(bf16[128,1536]{1,0:T(8,128)(2,1)} %get-tuple-element.63), channel_id=1, source_target_pairs={{0,32},{32,64},{64,96},{1,33},{33,65},{65,97},{2,34},{34,66},{66,9... | collective-permute-start | bytes 1179656 | tf_op jit(solution)/shard_map/ppermute | solution.py:37
  150.2 25.7 %collective-permute-start.43 = (bf16[128,1536]{1,0:T(8,128)(2,1)S(1)}, bf16[128,1536]{1,0:T(8,128)(2,1)S(1)}, u32[]{:S(2)}, u32[]{:S(2)}) collective-permute-start(bf16[128,1536]{1,0:T(8,128)(2,1)S(1)} %collective-permute-done.40.c3), channel_id=1, source_target_pairs={{0,1},{1,0},{2,3},{3,2},{4,5},{5,4},{6,7},{7,6},{8,9},{9,8},{10,11... | collective-permute-start | bytes 1179656 | tf_op jit(solution)/shard_map/ppermute | solution.py:37
  156.8 19.0 %collective-permute-start.42 = (bf16[128,1536]{1,0:T(8,128)(2,1)S(1)}, bf16[128,1536]{1,0:T(8,128)(2,1)S(1)}, u32[]{:S(2)}, u32[]{:S(2)}) collective-permute-start(bf16[128,1536]{1,0:T(8,128)(2,1)S(1)} %collective-permute-done.39.c2), channel_id=1, source_target_pairs={{0,1},{1,0},{2,3},{3,2},{4,5},{5,4},{6,7},{7,6},{8,9},{9,8},{10,11... | collective-permute-start | bytes 1179656 | tf_op jit(solution)/shard_map/ppermute | solution.py:37
  160.4 15.5 %collective-permute-start.41 = (bf16[128,1536]{1,0:T(8,128)(2,1)S(1)}, bf16[128,1536]{1,0:T(8,128)(2,1)S(1)}, u32[]{:S(2)}, u32[]{:S(2)}) collective-permute-start(bf16[128,1536]{1,0:T(8,128)(2,1)S(1)} %collective-permute-done.38.c1), channel_id=1, source_target_pairs={{0,1},{1,0},{2,3},{3,2},{4,5},{5,4},{6,7},{7,6},{8,9},{9,8},{10,11... | collective-permute-start | bytes 1179656 | tf_op jit(solution)/shard_map/ppermute | solution.py:37
  169.1 6.8 %collective-permute-start.37 = (bf16[128,512]{1,0:T(8,128)(2,1)S(1)}, bf16[128,512]{1,0:T(8,128)(2,1)S(1)}, u32[]{:S(2)}, u32[]{:S(2)}) collective-permute-start(bf16[128,512]{1,0:T(8,128)(2,1)S(1)} %copy-done.44), channel_id=1, source_target_pairs={{0,16},{16,0},{1,17},{17,1},{2,18},{18,2},{3,19},{19,3},{4,20},{20... | collective-permute-start | bytes 393224 | tf_op jit(solution)/shard_map/ppermute | solution.py:37
  174.9 11.2 %collective-permute-start.34 = (bf16[128,1536]{1,0:T(8,128)(2,1)}, bf16[128,1536]{1,0:T(8,128)(2,1)S(1)}, u32[]{:S(2)}, u32[]{:S(2)}) collective-permute-start(bf16[128,1536]{1,0:T(8,128)(2,1)} %shard_map.129.a0), channel_id=1, source_target_pairs={{0,2},{2,0},{1,3},{3,1},{4,6},{6,4},{5,7},{7,5},{8,10},{10,8},{9,1... | collective-permute-start | bytes 1179656 | tf_op jit(solution)/shard_map/ppermute | solution.py:37
  180.5 19.0 %all-to-all-start = ((bf16[8,4,96,128]{3,2,1,0:T(8,128)(2,1)}), bf16[8,4,96,128]{3,2,1,0:T(8,128)(2,1)S(1)}, u32[]{:S(2)}, u32[]{:S(2)}) async-start(bf16[8,4,96,128]{3,2,1,0:T(8,128)(2,1)} %shard_map.130), calls=%async_computation | async-start | bytes 1572864 | tf_op jit(solution)/shard_map/all_to_all | solution.py:41
  184.9 29.0 %collective-permute-start.35 = (bf16[128,1536]{1,0:T(8,128)(2,1)S(1)}, bf16[128,1536]{1,0:T(8,128)(2,1)S(1)}, u32[]{:S(2)}, u32[]{:S(2)}) collective-permute-start(bf16[128,1536]{1,0:T(8,128)(2,1)S(1)} %copy-done.1), channel_id=1, source_target_pairs={{0,1},{1,0},{2,3},{3,2},{4,5},{5,4},{6,7},{7,6},{8,9},{9,8},{10,11... | collective-permute-start | bytes 1179656 | tf_op jit(solution)/shard_map/ppermute | solution.py:37
  186.1 27.8 %collective-permute-start.36 = (bf16[128,1536]{1,0:T(8,128)(2,1)S(1)}, bf16[128,1536]{1,0:T(8,128)(2,1)S(1)}, u32[]{:S(2)}, u32[]{:S(2)}) collective-permute-start(bf16[128,1536]{1,0:T(8,128)(2,1)S(1)} %collective-permute-done.34.a1), channel_id=1, source_target_pairs={{0,1},{1,0},{2,3},{3,2},{4,5},{5,4},{6,7},{7,6},{8,9},{9,8},{10,11... | collective-permute-start | bytes 1179656 | tf_op jit(solution)/shard_map/ppermute | solution.py:37
  202.2 9.0 %collective-permute-start.44 = (f32[96,128]{1,0:T(8,128)}, f32[96,128]{1,0:T(8,128)S(1)}, u32[]{:S(2)}, u32[]{:S(2)}) collective-permute-start(f32[96,128]{1,0:T(8,128)} %get-tuple-element.69), channel_id=1, source_target_pairs={{0,96},{32,0},{64,32},{1,97},{33,1},{65,33},{2,98},{34,2},{66,34},... | collective-permute-start | bytes 147464 | tf_op jit(solution)/shard_map/ppermute | solution.py:37
  207.3 6.5 %collective-permute-start.45 = (f32[96,128]{1,0:T(8,128)}, f32[96,128]{1,0:T(8,128)S(1)}, u32[]{:S(2)}, u32[]{:S(2)}) collective-permute-start(f32[96,128]{1,0:T(8,128)} %get-tuple-element.70), channel_id=1, source_target_pairs={{0,64},{32,96},{64,0},{1,65},{33,97},{65,1},{2,66},{34,98},{66,2},... | collective-permute-start | bytes 147464 | tf_op jit(solution)/shard_map/ppermute | solution.py:37
  209.3 4.6 %collective-permute-start.46 = (f32[96,128]{1,0:T(8,128)}, f32[96,128]{1,0:T(8,128)S(1)}, u32[]{:S(2)}, u32[]{:S(2)}) collective-permute-start(f32[96,128]{1,0:T(8,128)} %get-tuple-element.71), channel_id=1, source_target_pairs={{0,32},{32,64},{64,96},{1,33},{33,65},{65,97},{2,34},{34,66},{66,9... | collective-permute-start | bytes 147464 | tf_op jit(solution)/shard_map/ppermute | solution.py:37
  (45 other events, 401.0 us)
